TPU v7x, 8 devices: a whole 2x2x1 slice. The times are simulated.
8 devices in a mesh: dp: 1 (over z), sp2: 2 (over y), sp: 4 (over x, core).
Axes of the slice: x: 2, y: 2, z: 1, core: 2. Of those that a mesh axis runs over, the one named last changes fastest.
Arguments:
- x: bfloat16 [32, 32, 256, 128], P('dp', 'sp', 'sp2')
- w_a: bfloat16 [3, 3, 3, 128, 128], replicated
- bn_a: float32 [3, 2, 128], replicated
- w_down: bfloat16 [3, 3, 128, 256], replicated
- bn_down: float32 [2, 256], replicated
- w_b: bfloat16 [2, 3, 3, 256, 256], replicated
- bn_b: float32 [2, 2, 256], replicated
Outputs:
- output: bfloat16 [32, 16, 128, 256], P('dp', 'sp', 'sp2')
All inputs are finite; a program needn't handle non-finite values.
Results may differ from a plain program's by a relative error of at most 0.00764817.
Values are sent between devices in bfloat16 or wider.
A program may use at most 1 GiB of HBM per device.

v0:
```python
import jax
import jax.numpy as jnp
from jax import lax
from jax.sharding import PartitionSpec as P

CONV_DIMS = ("NHWC", "HWIO", "NHWC")


def edge_extend(act_tile, axis_name, axis_len, line_dim, two_sided):
    tile_len = act_tile.shape[line_dim]
    first_line = lax.slice_in_dim(act_tile, 0, 1, axis=line_dim)
    from_next = lax.ppermute(first_line, axis_name, perm=[(device + 1, device) for device in range(axis_len - 1)])
    if two_sided:
        last_line = lax.slice_in_dim(act_tile, tile_len - 1, tile_len, axis=line_dim)
        from_prev = lax.ppermute(last_line, axis_name, perm=[(device, device + 1) for device in range(axis_len - 1)])
        return jnp.concatenate([from_prev, act_tile, from_next], axis=line_dim)
    return jnp.concatenate([act_tile, from_next], axis=line_dim)


def conv_bn(act_tile, weight, norm_pair, stride, grid_shape):
    rows_n, cols_n = grid_shape
    two_sided = stride == 1
    extended = edge_extend(act_tile, "sp", rows_n, 1, two_sided)
    extended = edge_extend(extended, "sp2", cols_n, 2, two_sided)
    pre_norm = lax.conv_general_dilated(extended, weight, (stride, stride), "VALID", dimension_numbers=CONV_DIMS, preferred_element_type=jnp.float32)
    moments = jnp.stack([jnp.sum(pre_norm, axis=(0, 1, 2)), jnp.sum(pre_norm * pre_norm, axis=(0, 1, 2))])
    moments = lax.psum(moments, ("sp2", "sp"))
    num_pos = pre_norm.shape[0] * pre_norm.shape[1] * pre_norm.shape[2] * rows_n * cols_n
    mean_val = moments[0] / num_pos
    var_val = moments[1] / num_pos - mean_val * mean_val
    normed = norm_pair[0] * (pre_norm - mean_val) * lax.rsqrt(var_val + 1e-5) + norm_pair[1]
    return jnp.maximum(normed, 0.0).astype(jnp.bfloat16)


def solution(mesh):
    grid_shape = (mesh.shape["sp"], mesh.shape["sp2"])

    def per_device(x, w_a, bn_a, w_down, bn_down, w_b, bn_b):
        act_tile = x
        for layer_idx in range(w_a.shape[0]):
            act_tile = conv_bn(act_tile, w_a[layer_idx], bn_a[layer_idx], 1, grid_shape)
        act_tile = conv_bn(act_tile, w_down, bn_down, 2, grid_shape)
        for layer_idx in range(w_b.shape[0]):
            act_tile = conv_bn(act_tile, w_b[layer_idx], bn_b[layer_idx], 1, grid_shape)
        return act_tile

    tile_spec = P("dp", "sp", "sp2", None)
    return jax.shard_map(per_device, mesh=mesh, in_specs=(tile_spec, P(), P(), P(), P(), P(), P()), out_specs=tile_spec, check_vma=False)
```

profile of v0, /device:TPU:0, one launch (start us, length us, event | category | flops | bytes accessed | tf_op | source)
XLA Modules:
  0.0 460.3 jit_solution(18311256306089102019)
XLA Ops:
  0.0 1.7 fusion.83
  1.8 0.7 copy.13
  2.4 2.8 collective-permute-start
  5.3 0.7 copy.14
  6.0 1.3 collective-permute-start.1
  7.5 1.1 constant_dynamic-update-slice_fusion.2
  8.5 12.2 %constant_dynamic-update-slice_fusion.1 = bf16[32,10,128,128]{3,0,2,1:T(8,128)(2,1)} fusion(bf16[32,10,128,128]{3,0,2,1:T(8,128)(2,1)} %constant_dynamic-update-slice_fusion.2, bf16[32,8,128,128]{3,2,1,0:T(8,128)(2,1)} %param.7), kind=kLoop, calls=%fused_computation.88 | loop fusion | bytes 16777216
  20.7 1.0 constant_dynamic-update-slice_fusion
  21.8 0.9 fusion.80
  22.7 4.3 collective-permute-start.2
  27.0 1.5 collective-permute-start.3
  29.0 4.3 collective-permute-done.3
  33.3 24.2 %fusion.76 = (f32[128]{0:T(128)S(1)}, f32[128]{0:T(128)S(1)}, f32[32,8,128,128]{3,0,2,1:T(8,128)}) fusion(bf16[3,3,3,128,128]{4,3,2,1,0:T(8,128)(2,1)S(1)} %copy-done.5, bf16[32,10,1,128]{3,0,2,1:T(8,128)(2,1)S(1)} %collective-permute-done.3, bf16[32,10,128,128]{3,0,2,1:T(8,128)(2,1)} %constant_dynamic-update-slice_fusion, ...), kind=kOutput, calls=%fused_computation.131 | convolution fusion | flops 9686908928 | bytes 27722752 | tf_op jit(solution)/shard_map/conv_general_dilated | solution.py:25
  57.6 33.8 %psum.42 = f32[2,128]{1,0:T(2,128)S(1)} all-reduce(f32[2,128]{1,0:T(2,128)S(1)} %pad_maximum_fusion.16), channel_id=1, replica_groups=mesh['dp'=1,'sp2'=2,'sp'=4] {'sp2','sp'}, use_global_device_ids=true, to_apply=%region_2.0 | all-reduce | flops 256 | bytes 2048 | tf_op jit(solution)/shard_map/psum | solution.py:27
  91.4 7.7 %maximum_convert_fusion.2 = bf16[32,8,128,128]{3,0,2,1:T(8,128)(2,1)S(1)} fusion(f32[32,8,128,128]{3,0,2,1:T(8,128)} %get-tuple-element.55, f32[128]{0:T(128)S(1)} %get-tuple-element.42, f32[128]{0:T(128)S(1)} %fusion.67, f32[128]{0:T(128)S(1)} %multiply_bitcast_fusion.2, f32[128]{0:T(128)S(1)} %get-tuple-element.43), kind=kLoop, calls=%fused_computation.4 | loop fusion | flops 25165824 | bytes 25167872 | tf_op jit(solution)/shard_map/convert_element_type | solution.py:32
  99.5 1.4 collective-permute-start.4
  100.8 1.3 collective-permute-start.5
  102.1 0.9 collective-permute-done.4
  103.0 4.8 %collective-permute-done.5 = bf16[32,1,128,128]{3,0,2,1:T(8,128)(2,1)S(1)} collective-permute-done((bf16[32,1,128,128]{3,0,2,1:T(8,128)(2,1)S(1)}, bf16[32,1,128,128]{3,0,2,1:T(8,128)(2,1)S(1)}, u32[]{:S(2)}, u32[]{:S(2)}) %collective-permute-start.5) | collective-permute-done | bytes 1048608 | tf_op jit(solution)/shard_map/ppermute | solution.py:12
  107.8 3.9 collective-permute-start.6
  111.8 1.5 collective-permute-start.7
  113.8 4.3 collective-permute-done.7
  118.1 22.5 %fusion.75 = (f32[128]{0:T(128)S(1)}, f32[128]{0:T(128)S(1)}, f32[32,8,128,128]{3,0,2,1:T(8,128)}) fusion(bf16[3,3,3,128,128]{4,3,2,1,0:T(8,128)(2,1)S(1)} %copy-done.5, bf16[32,10,1,128]{3,0,2,1:T(8,128)(2,1)S(1)} %collective-permute-done.7, bf16[32,1,128,128]{3,0,2,1:T(8,128)(2,1)S(1)} %collective-permute-done.5, ...), kind=kOutput, calls=%fused_computation.130 | convolution fusion | flops 9697558528 | bytes 27722752 | tf_op jit(solution)/shard_map/conv_general_dilated | solution.py:25
  140.6 32.0 %psum.43 = f32[2,128]{1,0:T(2,128)S(1)} all-reduce(f32[2,128]{1,0:T(2,128)S(1)} %pad_maximum_fusion.17), channel_id=1, replica_groups=mesh['dp'=1,'sp2'=2,'sp'=4] {'sp2','sp'}, use_global_device_ids=true, to_apply=%region_5.0 | all-reduce | flops 256 | bytes 2048 | tf_op jit(solution)/shard_map/psum | solution.py:27
  172.6 7.7 %maximum_convert_fusion.1 = bf16[32,8,128,128]{3,0,2,1:T(8,128)(2,1)S(1)} fusion(f32[32,8,128,128]{3,0,2,1:T(8,128)} %get-tuple-element.56, f32[128]{0:T(128)S(1)} %get-tuple-element.46, f32[128]{0:T(128)S(1)} %fusion.65, f32[128]{0:T(128)S(1)} %multiply_bitcast_fusion.1, f32[128]{0:T(128)S(1)} %get-tuple-element.44), kind=kLoop, calls=%fused_computation.2 | loop fusion | flops 25165824 | bytes 25167872 | tf_op jit(solution)/shard_map/convert_element_type | solution.py:32
  180.6 1.4 collective-permute-start.8
  182.0 1.3 collective-permute-start.9
  183.3 0.9 collective-permute-done.8
  184.2 4.8 %collective-permute-done.9 = bf16[32,1,128,128]{3,0,2,1:T(8,128)(2,1)S(1)} collective-permute-done((bf16[32,1,128,128]{3,0,2,1:T(8,128)(2,1)S(1)}, bf16[32,1,128,128]{3,0,2,1:T(8,128)(2,1)S(1)}, u32[]{:S(2)}, u32[]{:S(2)}) %collective-permute-start.9) | collective-permute-done | bytes 1048608 | tf_op jit(solution)/shard_map/ppermute | solution.py:12
  189.0 3.9 collective-permute-start.10
  192.9 1.7 collective-permute-start.11
  195.0 4.3 collective-permute-done.11
  199.3 22.5 %fusion.74 = (f32[128]{0:T(128)S(1)}, f32[128]{0:T(128)S(1)}, f32[32,8,128,128]{3,0,2,1:T(8,128)}) fusion(bf16[3,3,3,128,128]{4,3,2,1,0:T(8,128)(2,1)S(1)} %copy-done.5, bf16[32,10,1,128]{3,0,2,1:T(8,128)(2,1)S(1)} %collective-permute-done.11, bf16[32,1,128,128]{3,0,2,1:T(8,128)(2,1)S(1)} %collective-permute-done.9, ...), kind=kOutput, calls=%fused_computation.129 | convolution fusion | flops 9697558528 | bytes 27722752 | tf_op jit(solution)/shard_map/conv_general_dilated | solution.py:25
  221.7 32.0 %psum.44 = f32[2,128]{1,0:T(2,128)S(1)} all-reduce(f32[2,128]{1,0:T(2,128)S(1)} %pad_maximum_fusion.18), channel_id=1, replica_groups=mesh['dp'=1,'sp2'=2,'sp'=4] {'sp2','sp'}, use_global_device_ids=true, to_apply=%region_8.0 | all-reduce | flops 256 | bytes 2048 | tf_op jit(solution)/shard_map/psum | solution.py:27
  253.8 7.7 %maximum_convert_fusion = bf16[32,8,128,128]{3,0,2,1:T(8,128)(2,1)S(1)} fusion(f32[32,8,128,128]{3,0,2,1:T(8,128)} %get-tuple-element.57, f32[128]{0:T(128)S(1)} %get-tuple-element.45, f32[128]{0:T(128)S(1)} %fusion.63, f32[128]{0:T(128)S(1)} %multiply_bitcast_fusion, f32[128]{0:T(128)S(1)} %get-tuple-element.41), kind=kLoop, calls=%fused_computation | loop fusion | flops 25165824 | bytes 25167872 | tf_op jit(solution)/shard_map/convert_element_type | solution.py:32
  261.5 1.3 collective-permute-start.12
  262.8 3.3 collective-permute-done.12
  266.1 1.3 collective-permute-start.13
  267.4 4.9 %collective-permute-done.13 = bf16[32,9,1,128]{3,0,2,1:T(8,128)(2,1)S(1)} collective-permute-done((bf16[32,9,1,128]{3,0,2,1:T(8,128)(2,1)S(1)}, bf16[32,9,1,128]{3,0,2,1:T(8,128)(2,1)S(1)}, u32[]{:S(2)}, u32[]{:S(2)}) %collective-permute-start.13) | collective-permute-done | bytes 73760 | tf_op jit(solution)/shard_map/ppermute | solution.py:12
  272.3 8.0 %fusion.79 = (f32[256]{0:T(256)S(1)}, f32[256]{0:T(256)S(1)}, f32[32,4,64,256]{3,0,2,1:T(8,128)}) fusion(bf16[3,3,128,256]{3,2,1,0:T(8,128)(2,1)S(1)} %copy-done, bf16[32,9,1,128]{3,0,2,1:T(8,128)(2,1)S(1)} %collective-permute-done.13, bf16[32,1,128,128]{3,0,2,1:T(8,128)(2,1)S(1)} %collective-permute-done.12, ...), kind=kOutput, calls=%fused_computation.134 | convolution fusion | flops 4847640576 | bytes 18491392 | tf_op jit(solution)/shard_map/conv_general_dilated | solution.py:25
  280.3 32.4 %psum.45 = f32[2,256]{1,0:T(2,128)S(1)} all-reduce(f32[2,256]{1,0:T(2,128)S(1)} %pad_maximum_fusion.13), channel_id=1, replica_groups=mesh['dp'=1,'sp2'=2,'sp'=4] {'sp2','sp'}, use_global_device_ids=true, to_apply=%region_11.0 | all-reduce | flops 512 | bytes 4096 | tf_op jit(solution)/shard_map/psum | solution.py:27
  312.7 5.0 %maximum_convert_fusion.5 = bf16[32,4,64,256]{3,0,2,1:T(8,128)(2,1)S(1)} fusion(f32[32,4,64,256]{3,0,2,1:T(8,128)} %get-tuple-element.58, f32[256]{0:T(256)S(1)} %bitcast.99, f32[256]{0:T(256)S(1)} %add_rsqrt_fusion.2, f32[256]{0:T(256)S(1)} %bitcast.93, f32[256]{0:T(256)S(1)} %bitcast.98), kind=kLoop, calls=%fused_computation.42 | loop fusion | flops 12582912 | bytes 12587008 | tf_op jit(solution)/shard_map/convert_element_type | solution.py:32
  317.9 1.5 collective-permute-start.14
  319.4 1.3 collective-permute-start.15
  320.7 0.9 collective-permute-done.14
  321.6 4.8 %collective-permute-done.15 = bf16[32,1,64,256]{3,0,2,1:T(8,128)(2,1)S(1)} collective-permute-done((bf16[32,1,64,256]{3,0,2,1:T(8,128)(2,1)S(1)}, bf16[32,1,64,256]{3,0,2,1:T(8,128)(2,1)S(1)}, u32[]{:S(2)}, u32[]{:S(2)}) %collective-permute-start.15) | collective-permute-done | bytes 1048608 | tf_op jit(solution)/shard_map/ppermute | solution.py:12
  326.4 3.9 collective-permute-start.16
  330.3 1.3 collective-permute-start.17
  331.6 0.9 collective-permute-done.16
  332.5 4.3 collective-permute-done.17
  336.8 12.8 %fusion.78 = (f32[256]{0:T(256)S(1)}, f32[256]{0:T(256)S(1)}, f32[32,4,64,256]{3,0,2,1:T(8,128)}) fusion(bf16[2,3,3,256,256]{4,3,2,1,0:T(8,128)(2,1)S(1)} %copy-done.4, bf16[32,6,1,256]{3,0,2,1:T(8,128)(2,1)S(1)} %collective-permute-done.17, bf16[32,1,64,256]{3,0,2,1:T(8,128)(2,1)S(1)} %collective-permute-done.15, ...), kind=kOutput, calls=%fused_computation.133 | convolution fusion | flops 9682944000 | bytes 16058368 | tf_op jit(solution)/shard_map/conv_general_dilated | solution.py:25
  349.7 32.0 %psum.46 = f32[2,256]{1,0:T(2,128)S(1)} all-reduce(f32[2,256]{1,0:T(2,128)S(1)} %pad_maximum_fusion.14), channel_id=1, replica_groups=mesh['dp'=1,'sp2'=2,'sp'=4] {'sp2','sp'}, use_global_device_ids=true, to_apply=%region_14.0 | all-reduce | flops 512 | bytes 4096 | tf_op jit(solution)/shard_map/psum | solution.py:27
  381.7 5.0 %maximum_convert_fusion.4 = bf16[32,4,64,256]{3,0,2,1:T(8,128)(2,1)S(1)} fusion(f32[32,4,64,256]{3,0,2,1:T(8,128)} %get-tuple-element.59, f32[256]{0:T(256)S(1)} %bitcast.103, f32[256]{0:T(256)S(1)} %add_rsqrt_fusion.1, f32[256]{0:T(256)S(1)} %bitcast.97, f32[256]{0:T(256)S(1)} %bitcast.102), kind=kLoop, calls=%fused_computation.40 | loop fusion | flops 12582912 | bytes 12587008 | tf_op jit(solution)/shard_map/convert_element_type | solution.py:32
  386.9 1.4 collective-permute-start.18
  388.2 1.3 collective-permute-start.19
  389.5 0.9 collective-permute-done.18
  390.4 4.8 %collective-permute-done.19 = bf16[32,1,64,256]{3,0,2,1:T(8,128)(2,1)S(1)} collective-permute-done((bf16[32,1,64,256]{3,0,2,1:T(8,128)(2,1)S(1)}, bf16[32,1,64,256]{3,0,2,1:T(8,128)(2,1)S(1)}, u32[]{:S(2)}, u32[]{:S(2)}) %collective-permute-start.19) | collective-permute-done | bytes 1048608 | tf_op jit(solution)/shard_map/ppermute | solution.py:12
  395.3 3.9 collective-permute-start.20
  399.2 1.5 collective-permute-start.21
  401.4 4.3 collective-permute-done.21
  405.7 12.8 %fusion.77 = (f32[256]{0:T(256)S(1)}, f32[256]{0:T(256)S(1)}, f32[32,4,64,256]{3,0,2,1:T(8,128)}) fusion(bf16[2,3,3,256,256]{4,3,2,1,0:T(8,128)(2,1)S(1)} %copy-done.4, bf16[32,6,1,256]{3,0,2,1:T(8,128)(2,1)S(1)} %collective-permute-done.21, bf16[32,1,64,256]{3,0,2,1:T(8,128)(2,1)S(1)} %collective-permute-done.19, ...), kind=kOutput, calls=%fused_computation.132 | convolution fusion | flops 9682944000 | bytes 16058368 | tf_op jit(solution)/shard_map/conv_general_dilated | solution.py:25
  418.6 32.0 %psum.47 = f32[2,256]{1,0:T(2,128)S(1)} all-reduce(f32[2,256]{1,0:T(2,128)S(1)} %pad_maximum_fusion.15), channel_id=1, replica_groups=mesh['dp'=1,'sp2'=2,'sp'=4] {'sp2','sp'}, use_global_device_ids=true, to_apply=%region_17.0 | all-reduce | flops 512 | bytes 4096 | tf_op jit(solution)/shard_map/psum | solution.py:27
  450.6 5.0 %maximum_convert_fusion.3 = bf16[32,4,64,256]{3,0,2,1:T(8,128)(2,1)S(1)} fusion(f32[32,4,64,256]{3,0,2,1:T(8,128)} %get-tuple-element.60, f32[256]{0:T(256)S(1)} %bitcast.101, f32[256]{0:T(256)S(1)} %add_rsqrt_fusion, f32[256]{0:T(256)S(1)} %bitcast.95, f32[256]{0:T(256)S(1)} %bitcast.100), kind=kLoop, calls=%fused_computation.38 | loop fusion | flops 12582912 | bytes 12587008 | tf_op jit(solution)/shard_map/convert_element_type | solution.py:32
  455.6 4.5 copy.11
  (49 shorter events, 3.7 us)
Async XLA Ops:
  0.0 272.3 %copy-start = (bf16[3,3,128,256]{3,2,1,0:T(8,128)(2,1)S(1)}, bf16[3,3,128,256]{3,2,1,0:T(8,128)(2,1)}, u32[]{:S(2)}) copy-start(bf16[3,3,128,256]{3,2,1,0:T(8,128)(2,1)} %param.10) | copy-start | bytes 1769476
  2.4 5.0 %collective-permute-start = (bf16[32,1,128,128]{3,0,2,1:T(8,128)(2,1)S(1)}, bf16[32,1,128,128]{3,0,2,1:T(8,128)(2,1)S(1)}, u32[]{:S(2)}, u32[]{:S(2)}) collective-permute-start(bf16[32,1,128,128]{3,0,2,1:T(8,128)(2,1)S(1)} %copy.13), channel_id=1, source_target_pairs={{0,1},{1,2},{2,3},{4,5},{5,6},{6,7}} | collective-permute-start | bytes 3145736 | tf_op jit(solution)/shard_map/ppermute | solution.py:15
  6.0 14.8 %collective-permute-start.1 = (bf16[32,1,128,128]{3,0,2,1:T(8,128)(2,1)S(1)}, bf16[32,1,128,128]{3,0,2,1:T(8,128)(2,1)S(1)}, u32[]{:S(2)}, u32[]{:S(2)}) collective-permute-start(bf16[32,1,128,128]{3,0,2,1:T(8,128)(2,1)S(1)} %copy.14), channel_id=1, source_target_pairs={{1,0},{2,1},{3,2},{5,4},{6,5},{7,6}} | collective-permute-start | bytes 3145736 | tf_op jit(solution)/shard_map/ppermute | solution.py:12
  8.5 19.9 %copy-start.2 = (f32[3,2,128]{2,1,0:T(2,128)S(1)}, f32[3,2,128]{2,1,0:T(2,128)}, u32[]{:S(2)}) copy-start(f32[3,2,128]{2,1,0:T(2,128)} %param.9) | copy-start | bytes 9220
  8.5 24.8 %copy-start.5 = (bf16[3,3,3,128,128]{4,3,2,1,0:T(8,128)(2,1)S(1)}, bf16[3,3,3,128,128]{4,3,2,1,0:T(8,128)(2,1)}, u32[]{:S(2)}) copy-start(bf16[3,3,3,128,128]{4,3,2,1,0:T(8,128)(2,1)} %param.8) | copy-start | bytes 2654212
  22.7 6.3 %collective-permute-start.2 = (bf16[32,10,1,128]{3,0,2,1:T(8,128)(2,1)S(1)}, bf16[32,10,1,128]{3,0,2,1:T(8,128)(2,1)S(1)}, u32[]{:S(2)}, u32[]{:S(2)}) collective-permute-start(bf16[32,10,1,128]{3,0,2,1:T(8,128)(2,1)S(1)} %get-tuple-element.21), channel_id=1, source_target_pairs={{0,4},{1,5},{2,6},{3,7}} | collective-permute-start | bytes 245768 | tf_op jit(solution)/shard_map/ppermute | solution.py:15
  27.0 6.3 %collective-permute-start.3 = (bf16[32,10,1,128]{3,0,2,1:T(8,128)(2,1)S(1)}, bf16[32,10,1,128]{3,0,2,1:T(8,128)(2,1)S(1)}, u32[]{:S(2)}, u32[]{:S(2)}) collective-permute-start(bf16[32,10,1,128]{3,0,2,1:T(8,128)(2,1)S(1)} %get-tuple-element.22), channel_id=1, source_target_pairs={{4,0},{5,1},{6,2},{7,3}} | collective-permute-start | bytes 245768 | tf_op jit(solution)/shard_map/ppermute | solution.py:12
  99.5 3.6 collective-permute-start.4
  100.8 7.0 %collective-permute-start.5 = (bf16[32,1,128,128]{3,0,2,1:T(8,128)(2,1)S(1)}, bf16[32,1,128,128]{3,0,2,1:T(8,128)(2,1)S(1)}, u32[]{:S(2)}, u32[]{:S(2)}) collective-permute-start(bf16[32,1,128,128]{3,0,2,1:T(8,128)(2,1)S(1)} %get-tuple-element.26), channel_id=1, source_target_pairs={{1,0},{2,1},{3,2},{5,4},{6,5},{7,6}} | collective-permute-start | bytes 3145736 | tf_op jit(solution)/shard_map/ppermute | solution.py:12
  107.8 6.0 %collective-permute-start.6 = (bf16[32,10,1,128]{3,0,2,1:T(8,128)(2,1)S(1)}, bf16[32,10,1,128]{3,0,2,1:T(8,128)(2,1)S(1)}, u32[]{:S(2)}, u32[]{:S(2)}) collective-permute-start(bf16[32,10,1,128]{3,0,2,1:T(8,128)(2,1)S(1)} %get-tuple-element.19), channel_id=1, source_target_pairs={{0,4},{1,5},{2,6},{3,7}} | collective-permute-start | bytes 245768 | tf_op jit(solution)/shard_map/ppermute | solution.py:15
  111.8 6.3 %collective-permute-start.7 = (bf16[32,10,1,128]{3,0,2,1:T(8,128)(2,1)S(1)}, bf16[32,10,1,128]{3,0,2,1:T(8,128)(2,1)S(1)}, u32[]{:S(2)}, u32[]{:S(2)}) collective-permute-start(bf16[32,10,1,128]{3,0,2,1:T(8,128)(2,1)S(1)} %get-tuple-element.20), channel_id=1, source_target_pairs={{4,0},{5,1},{6,2},{7,3}} | collective-permute-start | bytes 245768 | tf_op jit(solution)/shard_map/ppermute | solution.py:12
  180.6 3.6 collective-permute-start.8
  182.0 7.0 %collective-permute-start.9 = (bf16[32,1,128,128]{3,0,2,1:T(8,128)(2,1)S(1)}, bf16[32,1,128,128]{3,0,2,1:T(8,128)(2,1)S(1)}, u32[]{:S(2)}, u32[]{:S(2)}) collective-permute-start(bf16[32,1,128,128]{3,0,2,1:T(8,128)(2,1)S(1)} %get-tuple-element.24), channel_id=1, source_target_pairs={{1,0},{2,1},{3,2},{5,4},{6,5},{7,6}} | collective-permute-start | bytes 3145736 | tf_op jit(solution)/shard_map/ppermute | solution.py:12
  189.0 6.0 %collective-permute-start.10 = (bf16[32,10,1,128]{3,0,2,1:T(8,128)(2,1)S(1)}, bf16[32,10,1,128]{3,0,2,1:T(8,128)(2,1)S(1)}, u32[]{:S(2)}, u32[]{:S(2)}) collective-permute-start(bf16[32,10,1,128]{3,0,2,1:T(8,128)(2,1)S(1)} %get-tuple-element.17), channel_id=1, source_target_pairs={{0,4},{1,5},{2,6},{3,7}} | collective-permute-start | bytes 245768 | tf_op jit(solution)/shard_map/ppermute | solution.py:15
  192.9 6.3 %collective-permute-start.11 = (bf16[32,10,1,128]{3,0,2,1:T(8,128)(2,1)S(1)}, bf16[32,10,1,128]{3,0,2,1:T(8,128)(2,1)S(1)}, u32[]{:S(2)}, u32[]{:S(2)}) collective-permute-start(bf16[32,10,1,128]{3,0,2,1:T(8,128)(2,1)S(1)} %get-tuple-element.18), channel_id=1, source_target_pairs={{4,0},{5,1},{6,2},{7,3}} | collective-permute-start | bytes 245768 | tf_op jit(solution)/shard_map/ppermute | solution.py:12
  261.4 6.0 %copy-start.3 = (f32[2,256]{1,0:T(2,128)S(1)}, f32[2,256]{1,0:T(2,128)}, u32[]{:S(2)}) copy-start(f32[2,256]{1,0:T(2,128)} %param.11) | copy-start | bytes 6148
  261.5 4.6 collective-permute-start.12
  266.1 6.2 %collective-permute-start.13 = (bf16[32,9,1,128]{3,0,2,1:T(8,128)(2,1)S(1)}, bf16[32,9,1,128]{3,0,2,1:T(8,128)(2,1)S(1)}, u32[]{:S(2)}, u32[]{:S(2)}) collective-permute-start(bf16[32,9,1,128]{3,0,2,1:T(8,128)(2,1)S(1)} %pad_maximum_fusion.12), channel_id=1, source_target_pairs={{4,0},{5,1},{6,2},{7,3}} | collective-permute-start | bytes 221192 | tf_op jit(solution)/shard_map/ppermute | solution.py:12
  317.7 13.9 %copy-start.1 = (f32[2,2,256]{2,1,0:T(2,128)S(1)}, f32[2,2,256]{2,1,0:T(2,128)}, u32[]{:S(2)}) copy-start(f32[2,2,256]{2,1,0:T(2,128)} %param.13) | copy-start | bytes 12292
  317.7 19.1 %copy-start.4 = (bf16[2,3,3,256,256]{4,3,2,1,0:T(8,128)(2,1)S(1)}, bf16[2,3,3,256,256]{4,3,2,1,0:T(8,128)(2,1)}, u32[]{:S(2)}) copy-start(bf16[2,3,3,256,256]{4,3,2,1,0:T(8,128)(2,1)} %param.12) | copy-start | bytes 7077892
  317.9 3.7 collective-permute-start.14
  319.4 7.0 %collective-permute-start.15 = (bf16[32,1,64,256]{3,0,2,1:T(8,128)(2,1)S(1)}, bf16[32,1,64,256]{3,0,2,1:T(8,128)(2,1)S(1)}, u32[]{:S(2)}, u32[]{:S(2)}) collective-permute-start(bf16[32,1,64,256]{3,0,2,1:T(8,128)(2,1)S(1)} %get-tuple-element.36), channel_id=1, source_target_pairs={{1,0},{2,1},{3,2},{5,4},{6,5},{7,6}} | collective-permute-start | bytes 3145736 | tf_op jit(solution)/shard_map/ppermute | solution.py:12
  326.4 6.1 %collective-permute-start.16 = (bf16[32,6,1,256]{3,0,2,1:T(8,128)(2,1)S(1)}, bf16[32,6,1,256]{3,0,2,1:T(8,128)(2,1)S(1)}, u32[]{:S(2)}, u32[]{:S(2)}) collective-permute-start(bf16[32,6,1,256]{3,0,2,1:T(8,128)(2,1)S(1)} %get-tuple-element.31), channel_id=1, source_target_pairs={{0,4},{1,5},{2,6},{3,7}} | collective-permute-start | bytes 294920 | tf_op jit(solution)/shard_map/ppermute | solution.py:15
  330.3 6.5 %collective-permute-start.17 = (bf16[32,6,1,256]{3,0,2,1:T(8,128)(2,1)S(1)}, bf16[32,6,1,256]{3,0,2,1:T(8,128)(2,1)S(1)}, u32[]{:S(2)}, u32[]{:S(2)}) collective-permute-start(bf16[32,6,1,256]{3,0,2,1:T(8,128)(2,1)S(1)} %get-tuple-element.32), channel_id=1, source_target_pairs={{4,0},{5,1},{6,2},{7,3}} | collective-permute-start | bytes 294920 | tf_op jit(solution)/shard_map/ppermute | solution.py:12
  386.9 3.6 collective-permute-start.18
  388.2 7.0 %collective-permute-start.19 = (bf16[32,1,64,256]{3,0,2,1:T(8,128)(2,1)S(1)}, bf16[32,1,64,256]{3,0,2,1:T(8,128)(2,1)S(1)}, u32[]{:S(2)}, u32[]{:S(2)}) collective-permute-start(bf16[32,1,64,256]{3,0,2,1:T(8,128)(2,1)S(1)} %get-tuple-element.34), channel_id=1, source_target_pairs={{1,0},{2,1},{3,2},{5,4},{6,5},{7,6}} | collective-permute-start | bytes 3145736 | tf_op jit(solution)/shard_map/ppermute | solution.py:12
  395.3 6.1 %collective-permute-start.20 = (bf16[32,6,1,256]{3,0,2,1:T(8,128)(2,1)S(1)}, bf16[32,6,1,256]{3,0,2,1:T(8,128)(2,1)S(1)}, u32[]{:S(2)}, u32[]{:S(2)}) collective-permute-start(bf16[32,6,1,256]{3,0,2,1:T(8,128)(2,1)S(1)} %get-tuple-element.29), channel_id=1, source_target_pairs={{0,4},{1,5},{2,6},{3,7}} | collective-permute-start | bytes 294920 | tf_op jit(solution)/shard_map/ppermute | solution.py:15
  399.2 6.5 %collective-permute-start.21 = (bf16[32,6,1,256]{3,0,2,1:T(8,128)(2,1)S(1)}, bf16[32,6,1,256]{3,0,2,1:T(8,128)(2,1)S(1)}, u32[]{:S(2)}, u32[]{:S(2)}) collective-permute-start(bf16[32,6,1,256]{3,0,2,1:T(8,128)(2,1)S(1)} %get-tuple-element.30), channel_id=1, source_target_pairs={{4,0},{5,1},{6,2},{7,3}} | collective-permute-start | bytes 294920 | tf_op jit(solution)/shard_map/ppermute | solution.py:12
where the time goes:
time: 468 us; the launch traced here: 460 us
  blocking collectives  194 us (41%)
  matrix products  103 us (22%)
  waiting for transfers between devices  55.7 us (12%)
  starting transfers between devices  44.8 us (10%)
  other arithmetic  38.2 us (8%)
  local copies, waits for them, and re-layouts  24 us (5%)
    psum x6, blocking collectives, conv_bn(): moments = lax.psum(moments, ('sp2', 'sp'))  194 us
    conv_general_dilated x6, matrix products, conv_bn(): lax.conv_general_dilated(extended, weight, (stride, stride), 'VALID', dim...  103 us
    ppermute x12, waiting for transfers between devices, edge_extend(): lax.ppermute(first_line, axis_name, perm=[(device + 1, device) for device...  48.9 us
    convert_element_type x6, other arithmetic, conv_bn(): return jnp.maximum(normed, 0.0).astype(jnp.bfloat16)  37.9 us
    ppermute x10, starting transfers between devices, edge_extend(): lax.ppermute(last_line, axis_name, perm=[(device, device + 1) for device...  28.3 us
    ppermute x12, starting transfers between devices, edge_extend(): lax.ppermute(first_line, axis_name, perm=[(device + 1, device) for device...  16.5 us
    unnamed x16, local copies, waits for them, and re-layouts  14.6 us
  transfers between devices with their start and end apart: 22, of which 21 were waited for; matrix products, arithmetic and copies ran while one was open for 3% of the time, Pallas kernels for 0%

commit v1 on v0

v1 whole, which is shorter than its diff:
```python
import functools

import jax
import jax.numpy as jnp
from jax import lax
from jax.experimental import pallas as pl
from jax.experimental.pallas import tpu as pltpu
from jax.sharding import PartitionSpec as P

EPS = 1e-5
NQ = 4
F32 = jnp.float32
BF16 = jnp.bfloat16


def stack_kernel(dims, x_hbm, wa_ref, bna_ref, wd_ref, bnd_ref, wb_ref, bnb_ref, y_ref,
                 xv, act, actb, z, stg, wp, wdp, cbuf_a, cbuf_b, stat,
                 x_sem, row_send, row_recv, misc_send, misc_recv, st_send, st_recv):
    imgs, rows, cols, ca, cb, la, lb, rows_n, cols_n = dims
    n_dev = rows_n * cols_n
    pairs = cols // 2
    rows_b, cols_b = rows // 2, cols // 2
    sp, sp2 = lax.axis_index("sp"), lax.axis_index("sp2")
    me = sp2 * rows_n + sp
    odd = sp % 2
    has_up, has_down = sp > 0, sp < rows_n - 1
    has = {0: has_up, 1: has_down}
    at_left = sp2 == 0

    def x_copy(r):
        return pltpu.make_async_copy(x_hbm.at[:, r], xv.at[:, r], x_sem.at[r])

    slow_row = odd * (rows - 1)
    fast_row = (rows - 1) - slow_row
    x_copy(slow_row).start()
    x_copy(fast_row).start()
    for r in range(1, rows - 1):
        x_copy(r).start()

    act[0] = jnp.zeros((cols + 2, imgs, ca), BF16)
    act[rows + 1] = jnp.zeros((cols + 2, imgs, ca), BF16)
    actb[0] = jnp.zeros((cols_b + 2, imgs, cb), BF16)
    actb[rows_b + 1] = jnp.zeros((cols_b + 2, imgs, cb), BF16)
    for r in range(1, rows + 1):
        for c in (0, cols + 1):
            act[r, c] = jnp.zeros((imgs, ca), BF16)
    for r in range(1, rows_b + 1):
        for c in (0, cols_b + 1):
            actb[r, c] = jnp.zeros((imgs, cb), BF16)

    barrier = pltpu.get_barrier_semaphore()

    def peer(d):
        q = (me + d) % n_dev
        return {"sp2": q // rows_n, "sp": q % rows_n}

    for d in range(1, n_dev):
        pl.semaphore_signal(barrier, inc=1, device_id=peer(d), device_id_type=pl.DeviceIdType.MESH)
    pl.semaphore_wait(barrier, n_dev - 1)

    def remote(src, dst, ssem, rsem, dev):
        return pltpu.make_async_remote_copy(src_ref=src, dst_ref=dst, send_sem=ssem, recv_sem=rsem,
                                            device_id=dev, device_id_type=pl.DeviceIdType.MESH)

    def vert(side):
        return {"sp": sp - 1 if side == 0 else sp + 1, "sp2": sp2}

    def diag(side):
        return {"sp": sp - 1 if side == 0 else sp + 1, "sp2": 1 - sp2}

    lateral = {"sp": sp, "sp2": 1 - sp2}

    def halo(buf, n_r, n_c):
        width = n_c // NQ
        edge_c = jnp.where(at_left, n_c, 1)
        halo_c = jnp.where(at_left, 0, n_c + 1)
        mine = (1, n_r)
        theirs = (n_r + 1, 0)

        def row_piece(side, q):
            cut = pl.ds(1 + q * width, width)
            return remote(buf.at[mine[side], cut], buf.at[theirs[side], cut], row_send.at[side, q],
                          row_recv.at[1 - side, q], vert(side))

        def corner(side):
            return remote(buf.at[mine[side], edge_c], buf.at[theirs[side], halo_c], misc_send.at[side],
                          misc_recv.at[1 - side], diag(side))

        def side_col(src):
            return remote(src, buf.at[pl.ds(1, n_r), halo_c], misc_send.at[2], misc_recv.at[2], lateral)

        my_halo_c = jnp.where(at_left, n_c + 1, 0)
        lands = (0, n_r + 1)

        def row_landing(side, q):
            cut = pl.ds(1 + q * width, width)
            return remote(buf.at[mine[side], cut], buf.at[lands[side], cut], row_send.at[side, q],
                          row_recv.at[side, q], vert(side))

        def corner_landing(side):
            return remote(buf.at[mine[side], edge_c], buf.at[lands[side], my_halo_c], misc_send.at[side],
                          misc_recv.at[side], diag(side))

        def side_landing(src):
            return remote(src, buf.at[pl.ds(1, n_r), my_halo_c], misc_send.at[2], misc_recv.at[2], lateral)

        return row_piece, corner, side_col, row_landing, corner_landing, side_landing

    def by_side(side_pred, fn):
        for side in (0, 1):
            pl.when(jnp.logical_and(side_pred(side), has[side]))(functools.partial(fn, side))

    is_slow = lambda side: odd == side
    is_fast = lambda side: odd != side

    def send_row(h, pred):
        def go(side):
            for q in range(NQ):
                h[0](side, q).start()
            h[1](side).start()
        by_side(pred, go)

    def wait_row(h, pred):
        def go(side):
            for q in range(NQ):
                h[3](side, q).wait_recv()
            h[4](side).wait_recv()
        by_side(pred, go)

    def drain_row(h, pred):
        def go(side):
            for q in range(NQ):
                h[0](side, q).wait_send()
            h[1](side).wait_send()
        by_side(pred, go)

    def all_sum(layer, s1, s2, fold):
        s1 = jnp.sum(s1, axis=0, keepdims=True)
        s2 = jnp.sum(s2, axis=0, keepdims=True)
        both = jnp.concatenate([s1, s2], axis=0)
        if fold:
            half = both[:, :ca] + both[:, ca:]
            both = jnp.concatenate([half, half], axis=1)
        stat[layer, me] = both
        sends = [remote(stat.at[layer, me], stat.at[layer, me], st_send.at[layer, d], st_recv.at[layer, d], peer(d))
                 for d in range(1, n_dev)]
        for s in sends:
            s.start()
        for d in range(1, n_dev):
            src = (me + n_dev - d) % n_dev
            remote(stat.at[layer, src], stat.at[layer, src], st_send.at[layer, d], st_recv.at[layer, d], peer(d)).wait_recv()
        for s in sends:
            s.wait_send()
        total = stat[layer, 0]
        for k in range(1, n_dev):
            total = total + stat[layer, k]
        return total

    def affine(total, num, gamma, beta):
        mean = total[0:1] / num
        var = total[1:2] / num - mean * mean
        return mean, gamma * lax.rsqrt(var + EPS), beta

    def load_x_row(r):
        x_copy(r).wait()

        def blk(c, carry):
            c0 = pl.multiple_of(c * 16, 16)
            for i in range(imgs):
                stg[pl.ds(i * 17, 16), :] = xv[i, r, pl.ds(c0, 16), :].astype(F32)
            for k in range(16):
                act[r + 1, 1 + c0 + k] = stg[pl.ds(k, imgs, stride=17), :].astype(BF16)
            return carry

        lax.fori_loop(0, cols // 16, blk, 0)

    def apply_bn(zz, aff):
        mean, scale, beta = aff
        return jnp.maximum((zz - mean) * scale + beta, 0.0).astype(BF16)

    JN = 8

    def norm_row_a(r, aff):
        def blk(c, carry):
            zz = z[r, pl.ds(pl.multiple_of(c * (JN * imgs), JN * imgs), JN * imgs), :]
            y = apply_bn(zz, aff).reshape(JN, imgs, 2 * ca)
            y = jnp.stack([y[:, :, :ca], y[:, :, ca:]], axis=1).reshape(2 * JN, imgs, ca)
            act[r + 1, pl.ds(1 + c * (2 * JN), 2 * JN)] = y
            return carry
        lax.fori_loop(0, pairs // JN, blk, 0)

    def norm_row_b(r, aff):
        def blk(c, carry):
            zz = z[r, pl.ds(pl.multiple_of(c * (JN * imgs), JN * imgs), JN * imgs), :]
            actb[r + 1, pl.ds(1 + c * JN, JN)] = apply_bn(zz, aff).reshape(JN, imgs, cb)
            return carry
        lax.fori_loop(0, cols_b // JN, blk, 0)

    def norm_col_a(aff):
        p = jnp.where(at_left, pairs - 1, 0)
        for r in range(rows):
            y = apply_bn(z[r, pl.ds(pl.multiple_of(p * imgs, imgs), imgs), :], aff)
            cbuf_a[r] = jnp.where(at_left, y[:, ca:], y[:, :ca])

    def norm_col_b(aff):
        p = jnp.where(at_left, cols_b - 1, 0)
        for r in range(rows_b):
            cbuf_b[r] = apply_bn(z[r, pl.ds(pl.multiple_of(p * imgs, imgs), imgs), :], aff)

    def put(r, c0, n_c, acc, s):
        z[r, c0 * imgs:(c0 + n_c) * imgs, :] = acc
        a3 = acc.reshape(n_c * imgs // 8, 8, acc.shape[-1])
        return s[0] + jnp.sum(a3, axis=0), s[1] + jnp.sum(a3 * a3, axis=0)

    JA = 16

    def conv_row_a(layer, r, s):
        for j0 in range(0, pairs, JA):
            parts = []
            for dy in range(3):
                v = act[r + dy, 2 * j0:2 * j0 + 2 * JA + 2].reshape(JA + 1, 2, imgs, ca)
                for c in range(4):
                    parts.append(v[c // 2:c // 2 + JA, c % 2].reshape(JA * imgs, ca))
            acc = jnp.dot(jnp.concatenate(parts, axis=1), wp[layer], preferred_element_type=F32)
            s = put(r, j0, JA, acc, s)
        return s

    JD = 16

    def conv_row_d(i, s):
        for c0 in range(0, cols_b, JD):
            first, last = [], []
            for dy in range(3):
                v = act[2 * i + dy + 1, 2 * c0 + 1:2 * c0 + 2 * JD + 2]
                a = v[:2 * JD].reshape(JD, 2, imgs, ca)
                b = v[1:].reshape(JD, 2, imgs, ca)
                first += [a[:, 0].reshape(JD * imgs, ca), a[:, 1].reshape(JD * imgs, ca)]
                last.append(b[:, 1].reshape(JD * imgs, ca))
            acc = jnp.dot(jnp.concatenate(first + last, axis=1), wdp[...], preferred_element_type=F32)
            s = put(i, c0, JD, acc, s)
        return s

    JB = 16

    def conv_row_b(layer, r, s):
        for c0 in range(0, cols_b, JB):
            parts = []
            for dy in range(3):
                for dx in range(3):
                    parts.append(actb[r + dy, c0 + dx:c0 + dx + JB].reshape(JB * imgs, cb))
            acc = jnp.dot(jnp.concatenate(parts, axis=1), wb_ref[layer], preferred_element_type=F32)
            s = put(r, c0, JB, acc, s)
        return s

    zero_stat = lambda: (jnp.zeros((8, 256), F32), jnp.zeros((8, 256), F32))

    for layer in range(la):
        for dy in range(3):
            for c in range(4):
                k0 = (dy * 4 + c) * ca
                zero = jnp.zeros((ca, ca), BF16)
                wp[layer, k0:k0 + ca, :ca] = wa_ref[layer, dy, c] if c < 3 else zero
                wp[layer, k0:k0 + ca, ca:] = wa_ref[layer, dy, c - 1] if c > 0 else zero
    order = [(dy, dx) for dy in range(3) for dx in range(2)] + [(dy, 2) for dy in range(3)]
    for k, (dy, dx) in enumerate(order):
        wdp[k * ca:(k + 1) * ca, :] = wd_ref[dy, dx]

    num_a = float(imgs * rows * cols * n_dev)
    num_b = float(imgs * rows_b * cols_b * n_dev)

    def dup(v):
        return jnp.concatenate([v, v], axis=1)

    ha = halo(act, rows, cols)
    aff = None
    for layer in range(la):
        if layer == 0:
            load_x_row(slow_row)
            send_row(ha, is_slow)
            load_x_row(fast_row)
            send_row(ha, is_fast)
            lax.fori_loop(1, rows - 1, lambda r, c: (load_x_row(r), c)[1], 0)
            edge_c = jnp.where(at_left, cols, 1)
            col_src = act.at[pl.ds(1, rows), edge_c]
            ha[2](col_src).start()
        else:
            norm_row_a(slow_row, aff)
            norm_col_a(aff)
            send_row(ha, is_slow)
            norm_row_a(fast_row, aff)
            send_row(ha, is_fast)
            col_src = cbuf_a
            ha[2](col_src).start()
            lax.fori_loop(1, rows - 1, lambda r, c: (norm_row_a(r, aff), c)[1], 0)
        ha[5](col_src).wait_recv()

        def step(k, s):
            @pl.when(k == rows - 1)
            def _():
                wait_row(ha, is_fast)

            @pl.when(k == rows)
            def _():
                wait_row(ha, is_slow)

            r = jnp.where(k == rows - 1, fast_row, jnp.where(k == rows, slow_row, k))
            return conv_row_a(layer, r, s)

        s1, s2 = lax.fori_loop(1, rows + 1, step, zero_stat())
        total = all_sum(layer, s1, s2, True)
        drain_row(ha, is_slow)
        drain_row(ha, is_fast)
        ha[2](col_src).wait_send()
        aff = affine(total, num_a, dup(bna_ref[layer, 0:1]), dup(bna_ref[layer, 1:2]))

    norm_row_a(0, aff)
    norm_col_a(aff)

    @pl.when(has_up)
    def _():
        for q in range(NQ):
            ha[0](0, q).start()

        @pl.when(sp2 == 1)
        def _():
            ha[1](0).start()

    @pl.when(sp2 == 1)
    def _():
        ha[2](cbuf_a).start()

    lax.fori_loop(1, rows, lambda r, c: (norm_row_a(r, aff), c)[1], 0)

    @pl.when(sp2 == 0)
    def _():
        ha[5](cbuf_a).wait_recv()

    def step_d(i, s):
        @pl.when(jnp.logical_and(i == rows_b - 1, has_down))
        def _():
            for q in range(NQ):
                ha[3](1, q).wait_recv()

            @pl.when(sp2 == 0)
            def _():
                ha[4](1).wait_recv()

        return conv_row_d(i, s)

    s1, s2 = lax.fori_loop(0, rows_b, step_d, zero_stat())
    total = all_sum(la, s1, s2, False)

    @pl.when(has_up)
    def _():
        for q in range(NQ):
            ha[0](0, q).wait_send()

        @pl.when(sp2 == 1)
        def _():
            ha[1](0).wait_send()

    @pl.when(sp2 == 1)
    def _():
        ha[2](cbuf_a).wait_send()

    aff = affine(total, num_b, bnd_ref[0:1], bnd_ref[1:2])

    hb = halo(actb, rows_b, cols_b)
    slow_b = odd * (rows_b - 1)
    fast_b = (rows_b - 1) - slow_b
    for layer in range(lb):
        norm_row_b(slow_b, aff)
        norm_col_b(aff)
        send_row(hb, is_slow)
        norm_row_b(fast_b, aff)
        send_row(hb, is_fast)
        hb[2](cbuf_b).start()
        lax.fori_loop(1, rows_b - 1, lambda r, c: (norm_row_b(r, aff), c)[1], 0)
        hb[5](cbuf_b).wait_recv()

        def step_b(k, s):
            @pl.when(k == rows_b - 1)
            def _():
                wait_row(hb, is_fast)

            @pl.when(k == rows_b)
            def _():
                wait_row(hb, is_slow)

            r = jnp.where(k == rows_b - 1, fast_b, jnp.where(k == rows_b, slow_b, k))
            return conv_row_b(layer, r, s)

        s1, s2 = lax.fori_loop(1, rows_b + 1, step_b, zero_stat())
        total = all_sum(la + 1 + layer, s1, s2, False)
        drain_row(hb, is_slow)
        drain_row(hb, is_fast)
        hb[2](cbuf_b).wait_send()
        aff = affine(total, num_b, bnb_ref[layer, 0:1], bnb_ref[layer, 1:2])

    def final_row(r, carry):
        def blk(c, carry):
            zz = z[r, pl.ds(pl.multiple_of(c * (JN * imgs), JN * imgs), JN * imgs), :]
            y_ref[r, pl.ds(c * JN, JN)] = apply_bn(zz, aff).reshape(JN, imgs, cb)
            return carry
        return lax.fori_loop(0, cols_b // JN, blk, carry)

    lax.fori_loop(0, rows_b, final_row, 0)


def solution(mesh):
    rows_n, cols_n = mesh.shape["sp"], mesh.shape["sp2"]

    def per_device(x, w_a, bn_a, w_down, bn_down, w_b, bn_b):
        imgs, rows, cols, ca = x.shape
        cb = w_down.shape[-1]
        la, lb = w_a.shape[0], w_b.shape[0]
        rows_b, cols_b = rows // 2, cols // 2
        dims = (imgs, rows, cols, ca, cb, la, lb, rows_n, cols_n)
        n_dev = rows_n * cols_n
        layers = la + 1 + lb
        vm = pl.BlockSpec(memory_space=pltpu.VMEM)
        dma = pltpu.SemaphoreType.DMA
        y = pl.pallas_call(
            functools.partial(stack_kernel, dims),
            out_shape=jax.ShapeDtypeStruct((rows_b, cols_b, imgs, cb), BF16),
            in_specs=[pl.BlockSpec(memory_space=pl.ANY)] + [vm] * 6,
            out_specs=vm,
            scratch_shapes=[
                pltpu.VMEM((imgs, rows, cols, ca), BF16),
                pltpu.VMEM((rows + 2, cols + 2, imgs, ca), BF16),
                pltpu.VMEM((rows_b + 2, cols_b + 2, imgs, cb), BF16),
                pltpu.VMEM((rows, cols // 2 * imgs, 2 * ca), F32),
                pltpu.VMEM((imgs * 17 + 16, ca), F32),
                pltpu.VMEM((la, 12 * ca, 2 * ca), BF16),
                pltpu.VMEM((9 * ca, cb), BF16),
                pltpu.VMEM((rows, imgs, ca), BF16),
                pltpu.VMEM((rows_b, imgs, cb), BF16),
                pltpu.VMEM((layers, n_dev, 2, 256), F32),
                dma((rows,)),
                dma((2, NQ)), dma((2, NQ)), dma((3,)), dma((3,)), dma((layers, n_dev)), dma((layers, n_dev)),
            ],
            compiler_params=pltpu.CompilerParams(
                collective_id=0, has_side_effects=True, vmem_limit_bytes=66_000_000),
            name="stack",
        )(x, w_a, bn_a, w_down, bn_down, w_b.reshape(lb, 9 * cb, cb), bn_b)
        return y.transpose(2, 0, 1, 3)

    tile_spec = P("dp", "sp", "sp2", None)
    return jax.shard_map(per_device, mesh=mesh, in_specs=(tile_spec, P(), P(), P(), P(), P(), P()),
                         out_specs=tile_spec, check_vma=False)
```

time: 468 us -> 143 us (0.31); the launches traced: 460 us -> 143 us
  blocking collectives: 194 us -> 0 us
  Pallas kernels: 0 us -> 137 us
  matrix products: 103 us -> 0 us
  waiting for transfers between devices: 55.7 us -> 0 us
  starting transfers between devices: 44.8 us -> 0 us
  other arithmetic: 38.2 us -> 0 us
  local copies, waits for them, and re-layouts: 24 us -> 6.57 us
    psum x6 -> x0, blocking collectives: 194 us -> none  [conv_bn(): moments = lax.psum(moments, ('sp2', 'sp'))]
    pallas_call x0 -> x1, Pallas kernels: none -> 137 us  [per_device(): pl.pallas_call(functools.partial(stack_kernel, dims), out_shape=jax.Shape...]
    conv_general_dilated x6 -> x0, matrix products: 103 us -> none  [conv_bn(): lax.conv_general_dilated(extended, weight, (stride, stride), 'VALID', dim...]
    ppermute x22 -> x0, waiting for transfers between devices: 55.7 us -> none  [the longest x12 48.9 us: edge_extend(): lax.ppermute(first_line, axis_name, perm=[(device + 1, device) for device...]
    ppermute x22 -> x0, starting transfers between devices: 44.8 us -> none  [the longest x10 28.3 us: edge_extend(): lax.ppermute(last_line, axis_name, perm=[(device, device + 1) for device...]
    convert_element_type x6 -> x0, other arithmetic: 37.9 us -> none  [conv_bn(): return jnp.maximum(normed, 0.0).astype(jnp.bfloat16)]
    unnamed x16 -> x0, local copies, waits for them, and re-layouts: 14.6 us -> none
    transpose x0 -> x1, local copies, waits for them, and re-layouts: none -> 6.57 us  [per_device(): return y.transpose(2, 0, 1, 3)]
  transfers between devices with their start and end apart: 22 -> 0, of which waited for: 21 -> 0; matrix products, arithmetic and copies ran while one was open for 3% -> 0% of each run, Pallas kernels for 0% -> 0%
where the time goes in v1:
time: 143 us
  Pallas kernels  137 us (96%)
  local copies, waits for them, and re-layouts  6.57 us (5%)
    pallas_call x1, Pallas kernels, per_device(): pl.pallas_call(functools.partial(stack_kernel, dims), out_shape=jax.Shape...  137 us
    transpose x1, local copies, waits for them, and re-layouts, per_device(): return y.transpose(2, 0, 1, 3)  6.57 us

profile of v1, /device:TPU:0, one launch (start us, length us, event | category | flops | bytes accessed | tf_op | source)
XLA Modules:
  0.0 143.1 jit_solution(11084569260345714003)
XLA Ops:
  0.0 136.6 %stack.1 = bf16[4,64,32,256]{3,2,1,0:T(8,128)(2,1)} custom-call(bf16[32,8,128,128]{3,2,1,0:T(8,128)(2,1)} %x_hbm.1, bf16[3,3,3,128,128]{4,3,2,1,0:T(8,128)(2,1)} %wa_ref.1, f32[3,2,128]{2,1,0:T(2,128)} %bna_ref.1, bf16[3,3,128,256]{3,2,1,0:T(8,128)(2,1)} %wd_ref.1, f32[2,256]{1,0:T(2,128)} %bnd_ref.1, bf16[2,2304,256]{2,1,0:T(8,128)(2,1)} %bitcast.3, ...), custom_call_target="tpu_custom_call" | custom-call | tf_op jit(solution)/shard_map/stack/pallas_call | solution.py:423
  136.6 6.6 %copy.8 = bf16[32,4,64,256]{3,2,1,0:T(8,128)(2,1)} copy(bf16[32,4,64,256]{3,0,2,1:T(8,128)(2,1)} %bitcast.2) | data formatting | bytes 8388608 | tf_op jit(solution)/shard_map/transpose | solution.py:446

commit v2 on v1

v2 whole, which is shorter than its diff:
```python
import functools

import jax
import jax.numpy as jnp
from jax import lax
from jax.experimental import pallas as pl
from jax.experimental.pallas import tpu as pltpu
from jax.sharding import PartitionSpec as P

EPS = 1e-5
NQ = 4
F32 = jnp.float32
BF16 = jnp.bfloat16


def stack_kernel(dims, x_hbm, wa_ref, bna_ref, wd_ref, bnd_ref, wb_ref, bnb_ref, y_ref,
                 xv, act, actb, z, stg, wp, wdp, wbv, cbuf_a, cbuf_b, stat,
                 x_sem, w_sem, row_send, row_recv, misc_send, misc_recv, st_send, st_recv):
    imgs, rows, cols, ca, cb, la, lb, rows_n, cols_n = dims
    n_dev = rows_n * cols_n
    pairs = cols // 2
    rows_b, cols_b = rows // 2, cols // 2
    sp, sp2 = lax.axis_index("sp"), lax.axis_index("sp2")
    me = sp2 * rows_n + sp
    odd = sp % 2
    has_up, has_down = sp > 0, sp < rows_n - 1
    has = {0: has_up, 1: has_down}
    at_left = sp2 == 0

    def x_copy(r):
        return pltpu.make_async_copy(x_hbm.at[:, r], xv.at[:, r], x_sem.at[r])

    slow_row = odd * (rows - 1)
    fast_row = (rows - 1) - slow_row
    x_copy(slow_row).start()
    x_copy(fast_row).start()
    for r in range(1, rows - 1):
        x_copy(r).start()

    order = [(dy, dx) for dy in range(3) for dx in range(2)] + [(dy, 2) for dy in range(3)]
    w_copies = [pltpu.make_async_copy(wd_ref.at[dy, dx], wdp.at[pl.ds(k * ca, ca)], w_sem.at[k])
                for k, (dy, dx) in enumerate(order)]
    w_copies.append(pltpu.make_async_copy(wb_ref, wbv, w_sem.at[9]))
    for c in w_copies:
        c.start()

    act[0] = jnp.zeros((cols + 2, imgs, ca), BF16)
    act[rows + 1] = jnp.zeros((cols + 2, imgs, ca), BF16)
    actb[0] = jnp.zeros((cols_b + 2, imgs, cb), BF16)
    actb[rows_b + 1] = jnp.zeros((cols_b + 2, imgs, cb), BF16)
    for r in range(1, rows + 1):
        for c in (0, cols + 1):
            act[r, c] = jnp.zeros((imgs, ca), BF16)
    for r in range(1, rows_b + 1):
        for c in (0, cols_b + 1):
            actb[r, c] = jnp.zeros((imgs, cb), BF16)

    barrier = pltpu.get_barrier_semaphore()

    def peer(d):
        q = (me + d) % n_dev
        return {"sp2": q // rows_n, "sp": q % rows_n}

    for d in range(1, n_dev):
        pl.semaphore_signal(barrier, inc=1, device_id=peer(d), device_id_type=pl.DeviceIdType.MESH)
    pl.semaphore_wait(barrier, n_dev - 1)

    def remote(src, dst, ssem, rsem, dev):
        return pltpu.make_async_remote_copy(src_ref=src, dst_ref=dst, send_sem=ssem, recv_sem=rsem,
                                            device_id=dev, device_id_type=pl.DeviceIdType.MESH)

    def vert(side):
        return {"sp": sp - 1 if side == 0 else sp + 1, "sp2": sp2}

    def diag(side):
        return {"sp": sp - 1 if side == 0 else sp + 1, "sp2": 1 - sp2}

    lateral = {"sp": sp, "sp2": 1 - sp2}

    def halo(buf, cbuf, n_r, n_c):
        ends = [(q + 1) * n_c // NQ + 2 for q in range(NQ - 1)] + [n_c + 1]
        cuts = [pl.ds(a, b - a) for a, b in zip([1] + ends[:-1], ends)]
        halo_c = jnp.where(at_left, 0, n_c + 1)
        mine, edge_r = (1, n_r), (0, n_r - 1)
        theirs = (n_r + 1, 0)

        def row_piece(side, q):
            cut = cuts[q]
            return remote(buf.at[mine[side], cut], buf.at[theirs[side], cut], row_send.at[side, q],
                          row_recv.at[1 - side, q], vert(side))

        def corner(side):
            return remote(cbuf.at[edge_r[side]], buf.at[theirs[side], halo_c], misc_send.at[side],
                          misc_recv.at[1 - side], diag(side))

        def side_col(src):
            return remote(src, buf.at[pl.ds(1, n_r), halo_c], misc_send.at[2], misc_recv.at[2], lateral)

        my_halo_c = jnp.where(at_left, n_c + 1, 0)
        lands = (0, n_r + 1)

        def row_landing(side, q):
            cut = cuts[q]
            return remote(buf.at[mine[side], cut], buf.at[lands[side], cut], row_send.at[side, q],
                          row_recv.at[side, q], vert(side))

        def corner_landing(side):
            return remote(cbuf.at[edge_r[side]], buf.at[lands[side], my_halo_c], misc_send.at[side],
                          misc_recv.at[side], diag(side))

        def side_landing(src):
            return remote(src, buf.at[pl.ds(1, n_r), my_halo_c], misc_send.at[2], misc_recv.at[2], lateral)

        return row_piece, corner, side_col, row_landing, corner_landing, side_landing

    def by_side(side_pred, fn):
        for side in (0, 1):
            pl.when(jnp.logical_and(side_pred(side), has[side]))(functools.partial(fn, side))

    is_slow = lambda side: odd == side
    is_fast = lambda side: odd != side

    def send_corner(h, pred):
        by_side(pred, lambda side: h[1](side).start())

    def produce_row(h, pred, make, tail=None):
        make(0)
        for q in range(1, NQ):
            make(q)
            by_side(pred, lambda side, q=q: h[0](side, q - 1).start())
        if tail is not None:
            tail()
        by_side(pred, lambda side: h[0](side, NQ - 1).start())

    def wait_row(h, pred, part, n_parts):
        def go(side):
            if part == 0:
                h[4](side).wait_recv()
            for q in range(part * NQ // n_parts, (part + 1) * NQ // n_parts):
                h[3](side, q).wait_recv()
        by_side(pred, go)

    def drain_row(h, pred):
        def go(side):
            for q in range(NQ):
                h[0](side, q).wait_send()
            h[1](side).wait_send()
        by_side(pred, go)

    def all_sum(layer, s1, s2, fold):
        s1 = jnp.sum(s1, axis=0, keepdims=True)
        s2 = jnp.sum(s2, axis=0, keepdims=True)
        both = jnp.concatenate([s1, s2], axis=0)
        if fold:
            half = both[:, :ca] + both[:, ca:]
            both = jnp.concatenate([half, half], axis=1)
        stat[layer, me] = both
        sends = [remote(stat.at[layer, me], stat.at[layer, me], st_send.at[layer, d], st_recv.at[layer, d], peer(d))
                 for d in range(1, n_dev)]
        for s in sends:
            s.start()
        for d in range(1, n_dev):
            src = (me + n_dev - d) % n_dev
            remote(stat.at[layer, src], stat.at[layer, src], st_send.at[layer, d], st_recv.at[layer, d], peer(d)).wait_recv()
        for s in sends:
            s.wait_send()
        total = stat[layer, 0]
        for k in range(1, n_dev):
            total = total + stat[layer, k]
        return total

    def affine(total, num, gamma, beta):
        mean = total[0:1] / num
        var = total[1:2] / num - mean * mean
        return mean, gamma * lax.rsqrt(var + EPS), beta

    def group(n, q):
        return (0, n) if q is None else (q * n // NQ, (q + 1) * n // NQ)

    def load_x_row(r, q=None):
        if q is None:
            x_copy(r).wait()
        load_x(r, *group(cols // 16, q))

    def load_x(r, lo, hi):
        def blk(c, carry):
            c0 = pl.multiple_of(c * 16, 16)
            for i in range(imgs):
                stg[0, pl.ds(i * 17, 16), :] = xv[i, r, pl.ds(c0, 16), :].astype(F32)
            for k in range(16):
                act[r + 1, 1 + c0 + k] = stg[0, pl.ds(k, imgs, stride=17), :].astype(BF16)
            return carry

        lax.fori_loop(lo, hi, blk, 0)

    def apply_bn(zz, aff):
        mean, scale, beta = aff
        return jnp.maximum((zz - mean) * scale + beta, 0.0)

    JN = 8

    def norm_row_a(r, aff, q=None):
        def blk(c, carry):
            zz = z[r, pl.ds(pl.multiple_of(c * (JN * imgs), JN * imgs), JN * imgs), :]
            y = apply_bn(zz, aff).astype(BF16).reshape(JN, imgs, 2 * ca)
            y = jnp.stack([y[:, :, :ca], y[:, :, ca:]], axis=1).reshape(2 * JN, imgs, ca)
            act[r + 1, pl.ds(1 + c * (2 * JN), 2 * JN)] = y
            return carry
        lax.fori_loop(*group(pairs // JN, q), blk, 0)

    def norm_row_b(r, aff, q=None):
        def blk(c, carry):
            zz = z[r, pl.ds(pl.multiple_of(c * (JN * imgs), JN * imgs), JN * imgs), :]
            actb[r + 1, pl.ds(1 + c * JN, JN)] = apply_bn(zz, aff).astype(BF16).reshape(JN, imgs, cb)
            return carry
        lax.fori_loop(*group(cols_b // JN, q), blk, 0)

    def norm_col_a(aff):
        p = jnp.where(at_left, pairs - 1, 0)
        for r in range(rows):
            y = apply_bn(z[r, pl.ds(pl.multiple_of(p * imgs, imgs), imgs), :], aff).astype(BF16)
            cbuf_a[r] = jnp.where(at_left, y[:, ca:], y[:, :ca])

    def norm_col_b(aff):
        p = jnp.where(at_left, cols_b - 1, 0)
        for r in range(rows_b):
            cbuf_b[r] = apply_bn(z[r, pl.ds(pl.multiple_of(p * imgs, imgs), imgs), :], aff).astype(BF16)

    def put(r, c0, n_c, acc, s):
        z[r, pl.ds(pl.multiple_of(c0 * imgs, 8 * imgs), n_c * imgs), :] = acc
        a3 = acc.reshape(n_c * imgs // 8, 8, acc.shape[-1])
        return s[0] + jnp.sum(a3, axis=0), s[1] + jnp.sum(a3 * a3, axis=0)

    JC = 16
    NC_A, NC_B = pairs // JC, cols_b // JC

    def conv_a(layer, r, j, s):
        parts = []
        for dy in range(3):
            v = act[r + dy, pl.ds(2 * JC * j, 2 * JC + 2)].reshape(JC + 1, 2, imgs, ca)
            for c in range(4):
                parts.append(v[c // 2:c // 2 + JC, c % 2].reshape(JC * imgs, ca))
        acc = jnp.dot(jnp.concatenate(parts, axis=1), wp[layer], preferred_element_type=F32)
        return put(r, JC * j, JC, acc, s)

    def conv_d(i, j, s):
        first, last = [], []
        for dy in range(3):
            v = act[2 * i + dy + 1, pl.ds(2 * JC * j + 1, 2 * JC + 1)]
            a = v[:2 * JC].reshape(JC, 2, imgs, ca)
            b = v[1:].reshape(JC, 2, imgs, ca)
            first += [a[:, 0].reshape(JC * imgs, ca), a[:, 1].reshape(JC * imgs, ca)]
            last.append(b[:, 1].reshape(JC * imgs, ca))
        acc = jnp.dot(jnp.concatenate(first + last, axis=1), wdp[...], preferred_element_type=F32)
        return put(i, JC * j, JC, acc, s)

    def conv_b(layer, r, j, s):
        parts = []
        for dy in range(3):
            for dx in range(3):
                parts.append(actb[r + dy, pl.ds(JC * j + dx, JC)].reshape(JC * imgs, cb))
        acc = jnp.dot(jnp.concatenate(parts, axis=1), wbv[layer], preferred_element_type=F32)
        return put(r, JC * j, JC, acc, s)

    zero_stat = lambda: (jnp.zeros((8, 256), F32), jnp.zeros((8, 256), F32))

    for layer in range(la):
        for dy in range(3):
            for c in range(4):
                k0 = (dy * 4 + c) * ca
                zero = jnp.zeros((ca, ca), BF16)
                wp[layer, k0:k0 + ca, :ca] = wa_ref[layer, dy, c] if c < 3 else zero
                wp[layer, k0:k0 + ca, ca:] = wa_ref[layer, dy, c - 1] if c > 0 else zero

    num_a = float(imgs * rows * cols * n_dev)
    num_b = float(imgs * rows_b * cols_b * n_dev)

    def dup(v):
        return jnp.concatenate([v, v], axis=1)

    ha = halo(act, cbuf_a, rows, cols)
    PA, PB = 2, 4

    def layer_a(layer, aff):
        @pl.when(layer == 0)
        def _():
            edge_b = jnp.where(at_left, cols // 16 - 1, 0)
            edge_c = jnp.where(at_left, cols, 1)
            for row, pred in ((slow_row, is_slow), (fast_row, is_fast)):
                x_copy(row).wait()
                load_x(row, edge_b, edge_b + 1)
                cbuf_a[row] = act[row + 1, edge_c]
                send_corner(ha, pred)
                produce_row(ha, pred, functools.partial(load_x_row, row))

            def inner(r, c):
                load_x_row(r)
                return c
            lax.fori_loop(1, rows - 1, inner, 0)
            for r in range(1, rows - 1):
                cbuf_a[r] = act[r + 1, edge_c]
            ha[2](cbuf_a).start()

        @pl.when(layer > 0)
        def _():
            norm_col_a(aff)
            norm_row_a(slow_row, aff, 0)
            send_corner(ha, is_slow)
            ha[2](cbuf_a).start()
            send_corner(ha, is_fast)
            produce_row(ha, is_slow, lambda q: norm_row_a(slow_row, aff, q) if q else None)
            produce_row(ha, is_fast, lambda q: norm_row_a(fast_row, aff, q))

            def inner(r, c):
                norm_row_a(r, aff)
                return c
            lax.fori_loop(1, rows - 1, inner, 0)

        def step(it, s):
            pl.when(it == 1)(lambda: ha[5](cbuf_a).wait_recv())
            for r in range(1, rows - 1):
                for u in range(NC_A // 2):
                    mid = NC_A // 4 + u
                    outer = u if u < NC_A // 4 else NC_A // 2 + u
                    s = conv_a(layer, r, jnp.where(it == 0, mid, outer), s)
            return s

        s = lax.fori_loop(0, 2, step, zero_stat())
        wait_row(ha, is_fast, 0, 1)
        for j in range(NC_A):
            s = conv_a(layer, fast_row, j, s)
        for part in range(PA):
            wait_row(ha, is_slow, part, PA)
            for j in range(part * NC_A // PA, (part + 1) * NC_A // PA):
                s = conv_a(layer, slow_row, j, s)
        total = all_sum(layer, *s, True)
        drain_row(ha, is_slow)
        drain_row(ha, is_fast)
        ha[2](cbuf_a).wait_send()
        return affine(total, num_a, dup(bna_ref[layer, 0:1]), dup(bna_ref[layer, 1:2]))

    no_aff = tuple(jnp.zeros((1, 2 * ca), F32) for _ in range(3))
    aff = lax.fori_loop(0, la, layer_a, no_aff)

    norm_col_a(aff)
    norm_row_a(0, aff, 0)

    @pl.when(sp2 == 1)
    def _():
        pl.when(has_up)(lambda: ha[1](0).start())
        ha[2](cbuf_a).start()

    for q in range(1, NQ):
        norm_row_a(0, aff, q)
        pl.when(has_up)(lambda q=q: ha[0](0, q - 1).start())
    pl.when(has_up)(lambda: ha[0](0, NQ - 1).start())

    def inner_d(r, c):
        norm_row_a(r, aff)
        return c

    lax.fori_loop(1, rows, inner_d, 0)
    for c in w_copies:
        c.wait()

    s = zero_stat()
    for i in range(rows_b - 1):
        for j in range(NC_B - 1):
            s = conv_d(i, j, s)
    pl.when(sp2 == 0)(lambda: ha[5](cbuf_a).wait_recv())
    for i in range(rows_b - 1):
        s = conv_d(i, NC_B - 1, s)
    for part in range(PB):
        @pl.when(has_down)
        def _():
            if part == 0:
                pl.when(sp2 == 0)(lambda: ha[4](1).wait_recv())
            for q in range(part * NQ // PB, (part + 1) * NQ // PB):
                ha[3](1, q).wait_recv()
        for j in range(part * NC_B // PB, (part + 1) * NC_B // PB):
            s = conv_d(rows_b - 1, j, s)
    total = all_sum(la, *s, False)

    @pl.when(has_up)
    def _():
        for q in range(NQ):
            ha[0](0, q).wait_send()
        pl.when(sp2 == 1)(lambda: ha[1](0).wait_send())

    @pl.when(sp2 == 1)
    def _():
        ha[2](cbuf_a).wait_send()

    aff = affine(total, num_b, bnd_ref[0:1], bnd_ref[1:2])

    hb = halo(actb, cbuf_b, rows_b, cols_b)
    slow_b = odd * (rows_b - 1)
    fast_b = (rows_b - 1) - slow_b

    def layer_b(layer, aff):
        norm_col_b(aff)
        norm_row_b(slow_b, aff, 0)
        send_corner(hb, is_slow)
        hb[2](cbuf_b).start()
        send_corner(hb, is_fast)
        produce_row(hb, is_slow, lambda q: norm_row_b(slow_b, aff, q) if q else None)
        produce_row(hb, is_fast, lambda q: norm_row_b(fast_b, aff, q))

        def inner(r, c):
            norm_row_b(r, aff)
            return c
        lax.fori_loop(1, rows_b - 1, inner, 0)
        s = zero_stat()
        for r in range(1, rows_b - 1):
            for j in range(1, NC_B - 1):
                s = conv_b(layer, r, j, s)
        hb[5](cbuf_b).wait_recv()
        wait_row(hb, is_fast, 0, 1)
        for r in range(1, rows_b - 1):
            for j in (0, NC_B - 1):
                s = conv_b(layer, r, j, s)
        for j in range(NC_B):
            s = conv_b(layer, fast_b, j, s)
        for part in range(PB):
            wait_row(hb, is_slow, part, PB)
            for j in range(part * NC_B // PB, (part + 1) * NC_B // PB):
                s = conv_b(layer, slow_b, j, s)
        total = all_sum(la + 1 + layer, *s, False)
        drain_row(hb, is_slow)
        drain_row(hb, is_fast)
        hb[2](cbuf_b).wait_send()
        return affine(total, num_b, bnb_ref[layer, 0:1], bnb_ref[layer, 1:2])

    aff = lax.fori_loop(0, lb, layer_b, aff)

    def final_row(r, carry):
        def blk(c, carry):
            c0 = pl.multiple_of(c * 16, 16)
            for k in range(16):
                y = apply_bn(z[r, pl.ds(pl.multiple_of(c0 * imgs + k * imgs, imgs), imgs), :], aff)
                for h in range(2):
                    stg[h, pl.ds(k * 33, imgs), :] = y[:, h * 128:(h + 1) * 128]
            for i in range(imgs):
                for h in range(2):
                    y_ref[i, r, pl.ds(c0, 16), h * 128:(h + 1) * 128] = stg[h, pl.ds(i, 16, stride=33), :].astype(BF16)
            return carry
        return lax.fori_loop(0, cols_b // 16, blk, carry)

    lax.fori_loop(0, rows_b, final_row, 0)


def solution(mesh):
    rows_n, cols_n = mesh.shape["sp"], mesh.shape["sp2"]

    def per_device(x, w_a, bn_a, w_down, bn_down, w_b, bn_b):
        imgs, rows, cols, ca = x.shape
        cb = w_down.shape[-1]
        la, lb = w_a.shape[0], w_b.shape[0]
        rows_b, cols_b = rows // 2, cols // 2
        dims = (imgs, rows, cols, ca, cb, la, lb, rows_n, cols_n)
        n_dev = rows_n * cols_n
        layers = la + 1 + lb
        vm = pl.BlockSpec(memory_space=pltpu.VMEM)
        hbm = pl.BlockSpec(memory_space=pl.ANY)
        dma = pltpu.SemaphoreType.DMA
        return pl.pallas_call(
            functools.partial(stack_kernel, dims),
            out_shape=jax.ShapeDtypeStruct((imgs, rows_b, cols_b, cb), BF16),
            in_specs=[hbm, vm, vm, hbm, vm, hbm, vm],
            out_specs=vm,
            scratch_shapes=[
                pltpu.VMEM((imgs, rows, cols, ca), BF16),
                pltpu.VMEM((rows + 2, cols + 2, imgs, ca), BF16),
                pltpu.VMEM((rows_b + 2, cols_b + 2, imgs, cb), BF16),
                pltpu.VMEM((rows, cols // 2 * imgs, 2 * ca), F32),
                pltpu.VMEM((2, imgs * 17 + 16, 128), F32),
                pltpu.VMEM((la, 12 * ca, 2 * ca), BF16),
                pltpu.VMEM((9 * ca, cb), BF16),
                pltpu.VMEM((lb, 9 * cb, cb), BF16),
                pltpu.VMEM((rows, imgs, ca), BF16),
                pltpu.VMEM((rows_b, imgs, cb), BF16),
                pltpu.VMEM((layers, n_dev, 2, 256), F32),
                dma((rows,)), dma((10,)),
                dma((2, NQ)), dma((2, NQ)), dma((3,)), dma((3,)), dma((layers, n_dev)), dma((layers, n_dev)),
            ],
            compiler_params=pltpu.CompilerParams(
                collective_id=0, has_side_effects=True, vmem_limit_bytes=66_000_000),
            name="stack",
        )(x, w_a, bn_a, w_down, bn_down, w_b.reshape(lb, 9 * cb, cb), bn_b)

    tile_spec = P("dp", "sp", "sp2", None)
    return jax.shard_map(per_device, mesh=mesh, in_specs=(tile_spec, P(), P(), P(), P(), P(), P()),
                         out_specs=tile_spec, check_vma=False)
```

time: 143 us -> 129 us (0.902)
  Pallas kernels: 137 us -> 124 us
  local copies, waits for them, and re-layouts: 6.57 us -> 4.79 us
    pallas_call x1, Pallas kernels: 137 us -> 124 us  [per_device(): pl.pallas_call(functools.partial(stack_kernel, dims), out_shape=jax.Shape...]
    transpose x1 -> x0, local copies, waits for them, and re-layouts: 6.57 us -> none  [per_device(): return y.transpose(2, 0, 1, 3)]
    unnamed x0 -> x1, local copies, waits for them, and re-layouts: none -> 4.79 us
where the time goes in v2:
time: 129 us
  Pallas kernels  124 us (96%)
  local copies, waits for them, and re-layouts  4.79 us (4%)
    pallas_call x1, Pallas kernels, per_device(): pl.pallas_call(functools.partial(stack_kernel, dims), out_shape=jax.Shape...  124 us
    unnamed x1, local copies, waits for them, and re-layouts  4.79 us

profile of v2, /device:TPU:0, one launch (start us, length us, event | category | flops | bytes accessed | tf_op | source)
XLA Modules:
  0.0 129.2 jit_solution(16303764402459831197)
XLA Ops:
  0.0 124.4 %stack.1 = bf16[32,4,64,256]{3,2,1,0:T(8,128)(2,1)} custom-call(bf16[32,8,128,128]{3,2,1,0:T(8,128)(2,1)} %x_hbm.1, bf16[3,3,3,128,128]{4,3,2,1,0:T(8,128)(2,1)} %wa_ref.1, f32[3,2,128]{2,1,0:T(2,128)} %bna_ref.1, bf16[3,3,128,256]{3,2,1,0:T(8,128)(2,1)} %wd_ref.1, f32[2,256]{1,0:T(2,128)} %bnd_ref.1, bf16[2,2304,256]{2,1,0:T(8,128)(2,1)} %bitcast.1, ...), custom_call_target="tpu_custom_call" | custom-call | tf_op jit(solution)/shard_map/stack/pallas_call | solution.py:466
  124.4 4.8 %copy.9 = bf16[32,4,64,256]{3,2,1,0:T(8,128)(2,1)} copy(bf16[32,4,64,256]{3,2,1,0:T(8,128)(2,1)} %stack.1) | data formatting | bytes 8388608

commit v3 on v2

--- a/solution.py
+++ b/solution.py
@@ -8,13 +8,14 @@
 from jax.sharding import PartitionSpec as P
 
 EPS = 1e-5
-NQ = 4
+FRAC = (2, 4, 6, 7, 8)
+NQ = len(FRAC)
 F32 = jnp.float32
 BF16 = jnp.bfloat16
 
 
-def stack_kernel(dims, x_hbm, wa_ref, bna_ref, wd_ref, bnd_ref, wb_ref, bnb_ref, y_ref,
-                 xv, act, actb, z, stg, wp, wdp, wbv, cbuf_a, cbuf_b, stat,
+def stack_kernel(dims, x_hbm, wa_hbm, bna_hbm, wd_ref, bnd_hbm, wb_ref, bnb_hbm, y_ref,
+                 wa_ref, bna_ref, bnd_ref, bnb_ref, xv, act, actb, z, stg, wp, wdp, wbv, cbuf_a, cbuf_b, stat,
                  x_sem, w_sem, row_send, row_recv, misc_send, misc_recv, st_send, st_recv):
     imgs, rows, cols, ca, cb, la, lb, rows_n, cols_n = dims
     n_dev = rows_n * cols_n
@@ -37,6 +38,11 @@
     for r in range(1, rows - 1):
         x_copy(r).start()
 
+    early = [pltpu.make_async_copy(a, b, w_sem.at[10 + k]) for k, (a, b) in enumerate(
+        ((wa_hbm, wa_ref), (bna_hbm, bna_ref), (bnd_hbm, bnd_ref), (bnb_hbm, bnb_ref)))]
+    for c in early:
+        c.start()
+
     order = [(dy, dx) for dy in range(3) for dx in range(2)] + [(dy, 2) for dy in range(3)]
     w_copies = [pltpu.make_async_copy(wd_ref.at[dy, dx], wdp.at[pl.ds(k * ca, ca)], w_sem.at[k])
                 for k, (dy, dx) in enumerate(order)]
@@ -78,7 +84,7 @@
     lateral = {"sp": sp, "sp2": 1 - sp2}
 
     def halo(buf, cbuf, n_r, n_c):
-        ends = [(q + 1) * n_c // NQ + 2 for q in range(NQ - 1)] + [n_c + 1]
+        ends = [f * n_c // 8 + 2 for f in FRAC[:-1]] + [n_c + 1]
         cuts = [pl.ds(a, b - a) for a, b in zip([1] + ends[:-1], ends)]
         halo_c = jnp.where(at_left, 0, n_c + 1)
         mine, edge_r = (1, n_r), (0, n_r - 1)
@@ -132,11 +138,11 @@
             tail()
         by_side(pred, lambda side: h[0](side, NQ - 1).start())
 
-    def wait_row(h, pred, part, n_parts):
+    def wait_row(h, pred, first, pieces):
         def go(side):
-            if part == 0:
+            if first:
                 h[4](side).wait_recv()
-            for q in range(part * NQ // n_parts, (part + 1) * NQ // n_parts):
+            for q in pieces:
                 h[3](side, q).wait_recv()
         by_side(pred, go)
 
@@ -172,39 +178,41 @@
     def affine(total, num, gamma, beta):
         mean = total[0:1] / num
         var = total[1:2] / num - mean * mean
-        return mean, gamma * lax.rsqrt(var + EPS), beta
+        scale = gamma * lax.rsqrt(var + EPS)
+        return scale, beta - mean * scale, jnp.zeros_like(beta)
 
     def group(n, q):
-        return (0, n) if q is None else (q * n // NQ, (q + 1) * n // NQ)
-
-    def load_x_row(r, q=None):
-        if q is None:
-            x_copy(r).wait()
-        load_x(r, *group(cols // 16, q))
-
-    def load_x(r, lo, hi):
+        return (0, n) if q is None else (((0,) + FRAC)[q] * n // 8, FRAC[q] * n // 8)
+
+    def load_x_row(r):
+        x_copy(r).wait()
+
         def blk(c, carry):
             c0 = pl.multiple_of(c * 16, 16)
             for i in range(imgs):
                 stg[0, pl.ds(i * 17, 16), :] = xv[i, r, pl.ds(c0, 16), :].astype(F32)
             for k in range(16):
-                act[r + 1, 1 + c0 + k] = stg[0, pl.ds(k, imgs, stride=17), :].astype(BF16)
+                z[r, pl.ds(pl.multiple_of(c * (8 * imgs), 8 * imgs) + (k // 2) * imgs, imgs),
+                  (k % 2) * ca:(k % 2 + 1) * ca] = stg[0, pl.ds(k, imgs, stride=17), :]
             return carry
 
-        lax.fori_loop(lo, hi, blk, 0)
+        lax.fori_loop(0, cols // 16, blk, 0)
 
     def apply_bn(zz, aff):
-        mean, scale, beta = aff
-        return jnp.maximum((zz - mean) * scale + beta, 0.0)
+        scale, shift, low = aff
+        return jnp.maximum(zz * scale + shift, low)
 
     JN = 8
+
+    def norm_a(r, p, aff):
+        off = p * imgs if isinstance(p, int) else pl.multiple_of(p * imgs, JN * imgs)
+        y = apply_bn(z[r, pl.ds(off, JN * imgs), :], aff).astype(BF16).reshape(JN, imgs, 2 * ca)
+        y = jnp.stack([y[:, :, :ca], y[:, :, ca:]], axis=1).reshape(2 * JN, imgs, ca)
+        act[r + 1, pl.ds(1 + 2 * p, 2 * JN)] = y
 
     def norm_row_a(r, aff, q=None):
         def blk(c, carry):
-            zz = z[r, pl.ds(pl.multiple_of(c * (JN * imgs), JN * imgs), JN * imgs), :]
-            y = apply_bn(zz, aff).astype(BF16).reshape(JN, imgs, 2 * ca)
-            y = jnp.stack([y[:, :, :ca], y[:, :, ca:]], axis=1).reshape(2 * JN, imgs, ca)
-            act[r + 1, pl.ds(1 + c * (2 * JN), 2 * JN)] = y
+            norm_a(r, c * JN, aff)
             return carry
         lax.fori_loop(*group(pairs // JN, q), blk, 0)
 
@@ -227,42 +235,51 @@
             cbuf_b[r] = apply_bn(z[r, pl.ds(pl.multiple_of(p * imgs, imgs), imgs), :], aff).astype(BF16)
 
     def put(r, c0, n_c, acc, s):
-        z[r, pl.ds(pl.multiple_of(c0 * imgs, 8 * imgs), n_c * imgs), :] = acc
+        off = c0 * imgs if isinstance(c0, int) else pl.multiple_of(c0 * imgs, 8 * imgs)
+        z[r, pl.ds(off, n_c * imgs), :] = acc
         a3 = acc.reshape(n_c * imgs // 8, 8, acc.shape[-1])
         return s[0] + jnp.sum(a3, axis=0), s[1] + jnp.sum(a3 * a3, axis=0)
 
     JC = 16
     NC_A, NC_B = pairs // JC, cols_b // JC
 
-    def conv_a(layer, r, j, s):
+    def conv_a(layer, r, c0, s, n=JC):
         parts = []
         for dy in range(3):
-            v = act[r + dy, pl.ds(2 * JC * j, 2 * JC + 2)].reshape(JC + 1, 2, imgs, ca)
+            v = act[r + dy, 2 * c0:2 * c0 + 2 * n + 2].reshape(n + 1, 2, imgs, ca)
             for c in range(4):
-                parts.append(v[c // 2:c // 2 + JC, c % 2].reshape(JC * imgs, ca))
+                parts.append(v[c // 2:c // 2 + n, c % 2].reshape(n * imgs, ca))
         acc = jnp.dot(jnp.concatenate(parts, axis=1), wp[layer], preferred_element_type=F32)
-        return put(r, JC * j, JC, acc, s)
-
-    def conv_d(i, j, s):
+        return put(r, c0, n, acc, s)
+
+    def conv_d(i, c0, s, n=JC):
         first, last = [], []
         for dy in range(3):
-            v = act[2 * i + dy + 1, pl.ds(2 * JC * j + 1, 2 * JC + 1)]
-            a = v[:2 * JC].reshape(JC, 2, imgs, ca)
-            b = v[1:].reshape(JC, 2, imgs, ca)
-            first += [a[:, 0].reshape(JC * imgs, ca), a[:, 1].reshape(JC * imgs, ca)]
-            last.append(b[:, 1].reshape(JC * imgs, ca))
+            v = act[2 * i + dy + 1, 2 * c0 + 1:2 * c0 + 2 * n + 2]
+            a = v[:2 * n].reshape(n, 2, imgs, ca)
+            b = v[1:].reshape(n, 2, imgs, ca)
+            first += [a[:, 0].reshape(n * imgs, ca), a[:, 1].reshape(n * imgs, ca)]
+            last.append(b[:, 1].reshape(n * imgs, ca))
         acc = jnp.dot(jnp.concatenate(first + last, axis=1), wdp[...], preferred_element_type=F32)
-        return put(i, JC * j, JC, acc, s)
-
-    def conv_b(layer, r, j, s):
+        return put(i, c0, n, acc, s)
+
+    def conv_b(layer, r, c0, s, n=JC):
         parts = []
         for dy in range(3):
             for dx in range(3):
-                parts.append(actb[r + dy, pl.ds(JC * j + dx, JC)].reshape(JC * imgs, cb))
+                parts.append(actb[r + dy, c0 + dx:c0 + dx + n].reshape(n * imgs, cb))
         acc = jnp.dot(jnp.concatenate(parts, axis=1), wbv[layer], preferred_element_type=F32)
-        return put(r, JC * j, JC, acc, s)
+        return put(r, c0, n, acc, s)
+
+    def slow_parts(n_c):
+        for q in range(NQ):
+            lo, hi = group(n_c, q)
+            yield q, [(lo, (hi - lo) // 2), ((lo + hi) // 2, (hi - lo) // 2)]
 
     zero_stat = lambda: (jnp.zeros((8, 256), F32), jnp.zeros((8, 256), F32))
+
+    for c in early:
+        c.wait()
 
     for layer in range(la):
         for dy in range(3):
@@ -279,68 +296,67 @@
         return jnp.concatenate([v, v], axis=1)
 
     ha = halo(act, cbuf_a, rows, cols)
-    PA, PB = 2, 4
+    halves = ((0, range(0, 2)), (1, range(2, NQ)))
 
     def layer_a(layer, aff):
-        @pl.when(layer == 0)
-        def _():
-            edge_b = jnp.where(at_left, cols // 16 - 1, 0)
-            edge_c = jnp.where(at_left, cols, 1)
-            for row, pred in ((slow_row, is_slow), (fast_row, is_fast)):
-                x_copy(row).wait()
-                load_x(row, edge_b, edge_b + 1)
-                cbuf_a[row] = act[row + 1, edge_c]
-                send_corner(ha, pred)
-                produce_row(ha, pred, functools.partial(load_x_row, row))
-
-            def inner(r, c):
-                load_x_row(r)
-                return c
-            lax.fori_loop(1, rows - 1, inner, 0)
-            for r in range(1, rows - 1):
-                cbuf_a[r] = act[r + 1, edge_c]
-            ha[2](cbuf_a).start()
-
-        @pl.when(layer > 0)
-        def _():
-            norm_col_a(aff)
-            norm_row_a(slow_row, aff, 0)
-            send_corner(ha, is_slow)
-            ha[2](cbuf_a).start()
-            send_corner(ha, is_fast)
-            produce_row(ha, is_slow, lambda q: norm_row_a(slow_row, aff, q) if q else None)
-            produce_row(ha, is_fast, lambda q: norm_row_a(fast_row, aff, q))
-
-            def inner(r, c):
-                norm_row_a(r, aff)
-                return c
-            lax.fori_loop(1, rows - 1, inner, 0)
-
-        def step(it, s):
-            pl.when(it == 1)(lambda: ha[5](cbuf_a).wait_recv())
-            for r in range(1, rows - 1):
-                for u in range(NC_A // 2):
-                    mid = NC_A // 4 + u
-                    outer = u if u < NC_A // 4 else NC_A // 2 + u
-                    s = conv_a(layer, r, jnp.where(it == 0, mid, outer), s)
-            return s
-
-        s = lax.fori_loop(0, 2, step, zero_stat())
-        wait_row(ha, is_fast, 0, 1)
+        norm_col_a(aff)
+        norm_row_a(slow_row, aff, 0)
+        send_corner(ha, is_slow)
+        ha[2](cbuf_a).start()
+        send_corner(ha, is_fast)
+        produce_row(ha, is_slow, lambda q: norm_row_a(slow_row, aff, q) if q else None)
+        produce_row(ha, is_fast, lambda q: norm_row_a(fast_row, aff, q))
+
+        s = zero_stat()
+        mid = [j * JC for j in range(NC_A // 4, NC_A - NC_A // 4)]
+        outer = [j * JC for j in range(NC_A) if j * JC not in mid]
+        inner = range(1, rows - 1)
+        first = range(mid[0] - JN, mid[-1] + JC + 1, JN)
+        rest = [(r, p) for r in inner for p in range(0, pairs, JN) if p not in first]
+        ready = {r: [(r, p) for p in first] for r in inner}
+        for pos, r in enumerate(inner):
+            if pos == 0:
+                start = sorted(ready[r] + ready[r + 1], key=lambda rp: rp[1])
+                now = [start[:8], start[8:]]
+                for rp in now[0]:
+                    norm_a(*rp, aff)
+            for u, c0 in enumerate(mid):
+                if pos == 0 and u == 1:
+                    for rp in now[1]:
+                        norm_a(*rp, aff)
+                s = conv_a(layer, r, c0, s)
+                todo = ready.get(r + 2)
+                if todo is None:
+                    todo, left = rest, len(inner) - pos
+                    take = -(-len(todo) // ((left - 1) * len(mid) + len(mid) - u))
+                else:
+                    take = -(-len(todo) // (len(mid) - u))
+                for rp in todo[:take]:
+                    norm_a(*rp, aff)
+                del todo[:take]
+
+        ha[5](cbuf_a).wait_recv()
+        wait_row(ha, is_fast, True, range(NQ))
+        for r in inner:
+            for c0 in outer:
+                s = conv_a(layer, r, c0, s)
         for j in range(NC_A):
-            s = conv_a(layer, fast_row, j, s)
-        for part in range(PA):
-            wait_row(ha, is_slow, part, PA)
-            for j in range(part * NC_A // PA, (part + 1) * NC_A // PA):
-                s = conv_a(layer, slow_row, j, s)
+            s = conv_a(layer, fast_row, j * JC, s)
+        for part, pieces in halves:
+            wait_row(ha, is_slow, part == 0, pieces)
+            for j in range(part * NC_A // 2, (part + 1) * NC_A // 2):
+                s = conv_a(layer, slow_row, j * JC, s)
         total = all_sum(layer, *s, True)
         drain_row(ha, is_slow)
         drain_row(ha, is_fast)
         ha[2](cbuf_a).wait_send()
         return affine(total, num_a, dup(bna_ref[layer, 0:1]), dup(bna_ref[layer, 1:2]))
 
-    no_aff = tuple(jnp.zeros((1, 2 * ca), F32) for _ in range(3))
-    aff = lax.fori_loop(0, la, layer_a, no_aff)
+    load_x_row(slow_row)
+    load_x_row(fast_row)
+    lax.fori_loop(1, rows - 1, lambda r, c: (load_x_row(r), c)[1], 0)
+    flat = jnp.zeros((1, 2 * ca), F32)
+    aff = lax.fori_loop(0, la, layer_a, (flat + 1.0, flat, flat - jnp.inf))
 
     norm_col_a(aff)
     norm_row_a(0, aff, 0)
@@ -365,20 +381,20 @@
 
     s = zero_stat()
     for i in range(rows_b - 1):
-        for j in range(NC_B - 1):
-            s = conv_d(i, j, s)
+        for c0 in range(0, cols_b - JC, JC):
+            s = conv_d(i, c0, s)
     pl.when(sp2 == 0)(lambda: ha[5](cbuf_a).wait_recv())
     for i in range(rows_b - 1):
-        s = conv_d(i, NC_B - 1, s)
-    for part in range(PB):
+        for c0 in (cols_b - JC, cols_b - JC // 2):
+            s = conv_d(i, c0, s, JC // 2)
+    for q, chunks in slow_parts(cols_b):
         @pl.when(has_down)
         def _():
-            if part == 0:
+            if q == 0:
                 pl.when(sp2 == 0)(lambda: ha[4](1).wait_recv())
-            for q in range(part * NQ // PB, (part + 1) * NQ // PB):
-                ha[3](1, q).wait_recv()
-        for j in range(part * NC_B // PB, (part + 1) * NC_B // PB):
-            s = conv_d(rows_b - 1, j, s)
+            ha[3](1, q).wait_recv()
+        for c0, n in chunks:
+            s = conv_d(rows_b - 1, c0, s, n)
     total = all_sum(la, *s, False)
 
     @pl.when(has_up)
@@ -412,19 +428,19 @@
         lax.fori_loop(1, rows_b - 1, inner, 0)
         s = zero_stat()
         for r in range(1, rows_b - 1):
-            for j in range(1, NC_B - 1):
-                s = conv_b(layer, r, j, s)
+            for c0 in range(JC, cols_b - JC, JC):
+                s = conv_b(layer, r, c0, s)
         hb[5](cbuf_b).wait_recv()
-        wait_row(hb, is_fast, 0, 1)
+        wait_row(hb, is_fast, True, range(NQ))
         for r in range(1, rows_b - 1):
-            for j in (0, NC_B - 1):
-                s = conv_b(layer, r, j, s)
-        for j in range(NC_B):
-            s = conv_b(layer, fast_b, j, s)
-        for part in range(PB):
-            wait_row(hb, is_slow, part, PB)
-            for j in range(part * NC_B // PB, (part + 1) * NC_B // PB):
-                s = conv_b(layer, slow_b, j, s)
+            for c0 in (0, cols_b - JC):
+                s = conv_b(layer, r, c0, s)
+        for c0 in range(0, cols_b, JC):
+            s = conv_b(layer, fast_b, c0, s)
+        for q, chunks in slow_parts(cols_b):
+            wait_row(hb, is_slow, q == 0, [q])
+            for c0, n in chunks:
+                s = conv_b(layer, slow_b, c0, s, n)
         total = all_sum(la + 1 + layer, *s, False)
         drain_row(hb, is_slow)
         drain_row(hb, is_fast)
@@ -465,10 +481,12 @@
         dma = pltpu.SemaphoreType.DMA
         return pl.pallas_call(
             functools.partial(stack_kernel, dims),
-            out_shape=jax.ShapeDtypeStruct((imgs, rows_b, cols_b, cb), BF16),
-            in_specs=[hbm, vm, vm, hbm, vm, hbm, vm],
+            out_shape=pltpu.VMEM((imgs, rows_b, cols_b, cb), BF16),
+            in_specs=[hbm] * 7,
             out_specs=vm,
             scratch_shapes=[
+                pltpu.VMEM(w_a.shape, BF16),
+                pltpu.VMEM(bn_a.shape, F32), pltpu.VMEM(bn_down.shape, F32), pltpu.VMEM(bn_b.shape, F32),
                 pltpu.VMEM((imgs, rows, cols, ca), BF16),
                 pltpu.VMEM((rows + 2, cols + 2, imgs, ca), BF16),
                 pltpu.VMEM((rows_b + 2, cols_b + 2, imgs, cb), BF16),
@@ -480,11 +498,11 @@
                 pltpu.VMEM((rows, imgs, ca), BF16),
                 pltpu.VMEM((rows_b, imgs, cb), BF16),
                 pltpu.VMEM((layers, n_dev, 2, 256), F32),
-                dma((rows,)), dma((10,)),
+                dma((rows,)), dma((14,)),
                 dma((2, NQ)), dma((2, NQ)), dma((3,)), dma((3,)), dma((layers, n_dev)), dma((layers, n_dev)),
             ],
             compiler_params=pltpu.CompilerParams(
-                collective_id=0, has_side_effects=True, vmem_limit_bytes=66_000_000),
+                collective_id=0, has_side_effects=True, vmem_limit_bytes=58_000_000),
             name="stack",
         )(x, w_a, bn_a, w_down, bn_down, w_b.reshape(lb, 9 * cb, cb), bn_b)
 

time: 129 us -> 119 us (0.922)
  Pallas kernels: 124 us -> 116 us
  local copies, waits for them, and re-layouts: 4.79 us -> 2.02 us
    pallas_call x1, Pallas kernels: 124 us -> 116 us  [per_device(): pl.pallas_call(functools.partial(stack_kernel, dims), out_shape=pltpu.VME...]
    unnamed x1, local copies, waits for them, and re-layouts: 4.79 us -> 2.02 us
where the time goes in v3:
time: 119 us; the launch traced here: 118 us
  Pallas kernels  116 us (97%)
  local copies, waits for them, and re-layouts  2.02 us (2%)
    pallas_call x1, Pallas kernels, per_device(): pl.pallas_call(functools.partial(stack_kernel, dims), out_shape=pltpu.VME...  116 us

profile of v3, /device:TPU:0, one launch (start us, length us, event | category | flops | bytes accessed | tf_op | source)
XLA Modules:
  0.0 118.4 jit_solution(17228232380133661547)
XLA Ops:
  0.0 116.4 %stack.1 = bf16[32,4,64,256]{3,2,1,0:T(8,128)(2,1)S(1)} custom-call(bf16[32,8,128,128]{3,2,1,0:T(8,128)(2,1)} %x_hbm.1, bf16[3,3,3,128,128]{4,3,2,1,0:T(8,128)(2,1)} %wa_hbm.1, f32[3,2,128]{2,1,0:T(2,128)} %bna_hbm.1, bf16[3,3,128,256]{3,2,1,0:T(8,128)(2,1)} %wd_ref.1, f32[2,256]{1,0:T(2,128)} %bnd_hbm.1, bf16[2,2304,256]{2,1,0:T(8,128)(2,1)} %bitcast.1, ...), custom_call_target="tpu_custom_call" | custom-call | tf_op jit(solution)/shard_map/stack/pallas_call | solution.py:482
  116.4 2.0 %copy.9 = bf16[32,4,64,256]{3,2,1,0:T(8,128)(2,1)} copy(bf16[32,4,64,256]{3,2,1,0:T(8,128)(2,1)S(1)} %stack.1) | data formatting | bytes 8388608

commit v4 on v3

--- a/solution.py
+++ b/solution.py
@@ -8,7 +8,7 @@
 from jax.sharding import PartitionSpec as P
 
 EPS = 1e-5
-FRAC = (2, 4, 6, 7, 8)
+FRAC = (1, 3, 5, 7, 8)
 NQ = len(FRAC)
 F32 = jnp.float32
 BF16 = jnp.bfloat16
@@ -16,7 +16,7 @@
 
 def stack_kernel(dims, x_hbm, wa_hbm, bna_hbm, wd_ref, bnd_hbm, wb_ref, bnb_hbm, y_ref,
                  wa_ref, bna_ref, bnd_ref, bnb_ref, xv, act, actb, z, stg, wp, wdp, wbv, cbuf_a, cbuf_b, stat,
-                 x_sem, w_sem, row_send, row_recv, misc_send, misc_recv, st_send, st_recv):
+                 zhalo, x_sem, w_sem, z_send, z_recv, row_send, row_recv, misc_send, misc_recv, st_send, st_recv):
     imgs, rows, cols, ca, cb, la, lb, rows_n, cols_n = dims
     n_dev = rows_n * cols_n
     pairs = cols // 2
@@ -129,13 +129,12 @@
     def send_corner(h, pred):
         by_side(pred, lambda side: h[1](side).start())
 
-    def produce_row(h, pred, make, tail=None):
+    def produce_row(h, pred, make, skip=0):
         make(0)
         for q in range(1, NQ):
             make(q)
-            by_side(pred, lambda side, q=q: h[0](side, q - 1).start())
-        if tail is not None:
-            tail()
+            if q > skip:
+                by_side(pred, lambda side, q=q: h[0](side, q - 1).start())
         by_side(pred, lambda side: h[0](side, NQ - 1).start())
 
     def wait_row(h, pred, first, pieces):
@@ -146,14 +145,24 @@
                 h[3](side, q).wait_recv()
         by_side(pred, go)
 
-    def drain_row(h, pred):
+    def drain_row(h, pred, skip=0):
         def go(side):
-            for q in range(NQ):
+            for q in range(skip, NQ):
                 h[0](side, q).wait_send()
             h[1](side).wait_send()
         by_side(pred, go)
 
-    def all_sum(layer, s1, s2, fold):
+    zn = (cols_b // 8 + 1) * imgs
+    slow_dev = sp + 2 * odd - 1
+    has_slow = jnp.logical_and(slow_dev >= 0, slow_dev < rows_n)
+    slow_up = jnp.logical_and(has_slow, odd == 0)
+    slow_down = jnp.logical_and(has_slow, odd == 1)
+
+    def z_copy(t, row):
+        return remote(z.at[row, pl.ds(0, zn)], zhalo.at[t], z_send.at[t], z_recv.at[t],
+                      {"sp": slow_dev, "sp2": sp2})
+
+    def all_sum(layer, s1, s2, fold, ahead=lambda: None):
         s1 = jnp.sum(s1, axis=0, keepdims=True)
         s2 = jnp.sum(s2, axis=0, keepdims=True)
         both = jnp.concatenate([s1, s2], axis=0)
@@ -165,6 +174,7 @@
                  for d in range(1, n_dev)]
         for s in sends:
             s.start()
+        ahead()
         for d in range(1, n_dev):
             src = (me + n_dev - d) % n_dev
             remote(stat.at[layer, src], stat.at[layer, src], st_send.at[layer, d], st_recv.at[layer, d], peer(d)).wait_recv()
@@ -296,7 +306,7 @@
         return jnp.concatenate([v, v], axis=1)
 
     ha = halo(act, cbuf_a, rows, cols)
-    halves = ((0, range(0, 2)), (1, range(2, NQ)))
+    halves = ((0, range(0, 3)), (1, range(3, NQ)))
 
     def layer_a(layer, aff):
         norm_col_a(aff)
@@ -346,7 +356,8 @@
             wait_row(ha, is_slow, part == 0, pieces)
             for j in range(part * NC_A // 2, (part + 1) * NC_A // 2):
                 s = conv_a(layer, slow_row, j * JC, s)
-        total = all_sum(layer, *s, True)
+        total = all_sum(layer, *s, True, lambda: pl.when(jnp.logical_and(slow_up, layer == la - 1))(
+            lambda: z_copy(0, 0).start()))
         drain_row(ha, is_slow)
         drain_row(ha, is_fast)
         ha[2](cbuf_a).wait_send()
@@ -366,9 +377,11 @@
         pl.when(has_up)(lambda: ha[1](0).start())
         ha[2](cbuf_a).start()
 
+    fast_up = jnp.logical_and(has_up, odd == 1)
+    fast_down = jnp.logical_and(has_down, odd == 0)
     for q in range(1, NQ):
         norm_row_a(0, aff, q)
-        pl.when(has_up)(lambda q=q: ha[0](0, q - 1).start())
+        pl.when(has_up if q > 1 else fast_up)(lambda q=q: ha[0](0, q - 1).start())
     pl.when(has_up)(lambda: ha[0](0, NQ - 1).start())
 
     def inner_d(r, c):
@@ -379,27 +392,37 @@
     for c in w_copies:
         c.wait()
 
+    pl.when(slow_up)(lambda: z_copy(0, 0).wait_send())
     s = zero_stat()
     for i in range(rows_b - 1):
         for c0 in range(0, cols_b - JC, JC):
             s = conv_d(i, c0, s)
+
+    @pl.when(slow_down)
+    def _():
+        z_copy(0, 0).wait_recv()
+        y = apply_bn(zhalo[0], aff).astype(BF16).reshape(zn // imgs, imgs, 2 * ca)
+        y = jnp.stack([y[:, :, :ca], y[:, :, ca:]], axis=1).reshape(2 * zn // imgs, imgs, ca)
+        act[rows + 1, 1:cols // 8 + 2] = y[:cols // 8 + 1]
+
     pl.when(sp2 == 0)(lambda: ha[5](cbuf_a).wait_recv())
     for i in range(rows_b - 1):
         for c0 in (cols_b - JC, cols_b - JC // 2):
             s = conv_d(i, c0, s, JC // 2)
     for q, chunks in slow_parts(cols_b):
-        @pl.when(has_down)
-        def _():
-            if q == 0:
-                pl.when(sp2 == 0)(lambda: ha[4](1).wait_recv())
-            ha[3](1, q).wait_recv()
+        if q == 0:
+            pl.when(jnp.logical_and(has_down, sp2 == 0))(lambda: ha[4](1).wait_recv())
+        pl.when(has_down if q else fast_down)(lambda: ha[3](1, q).wait_recv())
         for c0, n in chunks:
             s = conv_d(rows_b - 1, c0, s, n)
-    total = all_sum(la, *s, False)
+    slow_b = odd * (rows_b - 1)
+    total = all_sum(la, *s, False, lambda: pl.when(has_slow)(lambda: z_copy(1, slow_b).start()))
+
+    pl.when(fast_up)(lambda: ha[0](0, 0).wait_send())
 
     @pl.when(has_up)
     def _():
-        for q in range(NQ):
+        for q in range(1, NQ):
             ha[0](0, q).wait_send()
         pl.when(sp2 == 1)(lambda: ha[1](0).wait_send())
 
@@ -410,7 +433,6 @@
     aff = affine(total, num_b, bnd_ref[0:1], bnd_ref[1:2])
 
     hb = halo(actb, cbuf_b, rows_b, cols_b)
-    slow_b = odd * (rows_b - 1)
     fast_b = (rows_b - 1) - slow_b
 
     def layer_b(layer, aff):
@@ -419,7 +441,7 @@
         send_corner(hb, is_slow)
         hb[2](cbuf_b).start()
         send_corner(hb, is_fast)
-        produce_row(hb, is_slow, lambda q: norm_row_b(slow_b, aff, q) if q else None)
+        produce_row(hb, is_slow, lambda q: norm_row_b(slow_b, aff, q) if q else None, 1)
         produce_row(hb, is_fast, lambda q: norm_row_b(fast_b, aff, q))
 
         def inner(r, c):
@@ -430,6 +452,13 @@
         for r in range(1, rows_b - 1):
             for c0 in range(JC, cols_b - JC, JC):
                 s = conv_b(layer, r, c0, s)
+
+        def first_piece(side):
+            z_copy(1 + layer, slow_b).wait_send()
+            z_copy(1 + layer, slow_b).wait_recv()
+            y = apply_bn(zhalo[1 + layer], aff).astype(BF16).reshape(zn // imgs, imgs, cb)
+            actb[(0, rows_b + 1)[side], 1:zn // imgs + 1] = y
+        by_side(is_slow, first_piece)
         hb[5](cbuf_b).wait_recv()
         wait_row(hb, is_fast, True, range(NQ))
         for r in range(1, rows_b - 1):
@@ -438,11 +467,12 @@
         for c0 in range(0, cols_b, JC):
             s = conv_b(layer, fast_b, c0, s)
         for q, chunks in slow_parts(cols_b):
-            wait_row(hb, is_slow, q == 0, [q])
+            wait_row(hb, is_slow, q == 0, [q] if q else [])
             for c0, n in chunks:
                 s = conv_b(layer, slow_b, c0, s, n)
-        total = all_sum(la + 1 + layer, *s, False)
-        drain_row(hb, is_slow)
+        total = all_sum(la + 1 + layer, *s, False, lambda: pl.when(jnp.logical_and(has_slow, layer + 1 < lb))(
+            lambda: z_copy(2 + layer, slow_b).start()))
+        drain_row(hb, is_slow, 1)
         drain_row(hb, is_fast)
         hb[2](cbuf_b).wait_send()
         return affine(total, num_b, bnb_ref[layer, 0:1], bnb_ref[layer, 1:2])
@@ -450,17 +480,25 @@
     aff = lax.fori_loop(0, lb, layer_b, aff)
 
     def final_row(r, carry):
-        def blk(c, carry):
-            c0 = pl.multiple_of(c * 16, 16)
+        def half_block(c0, g):
             for k in range(16):
                 y = apply_bn(z[r, pl.ds(pl.multiple_of(c0 * imgs + k * imgs, imgs), imgs), :], aff)
                 for h in range(2):
-                    stg[h, pl.ds(k * 33, imgs), :] = y[:, h * 128:(h + 1) * 128]
+                    stg[g + h, pl.ds(k * 33, imgs), :] = y[:, h * 128:(h + 1) * 128]
+
+        def turn(c0, g):
             for i in range(imgs):
                 for h in range(2):
-                    y_ref[i, r, pl.ds(c0, 16), h * 128:(h + 1) * 128] = stg[h, pl.ds(i, 16, stride=33), :].astype(BF16)
+                    y_ref[i, r, pl.ds(c0, 16), h * 128:(h + 1) * 128] = stg[g + h, pl.ds(i, 16, stride=33), :].astype(BF16)
+
+        def blk(c, carry):
+            c0 = pl.multiple_of(c * 32, 32)
+            half_block(c0, 0)
+            half_block(c0 + 16, 2)
+            turn(c0, 0)
+            turn(pl.multiple_of(c0 + 16, 16), 2)
             return carry
-        return lax.fori_loop(0, cols_b // 16, blk, carry)
+        return lax.fori_loop(0, cols_b // 32, blk, carry)
 
     lax.fori_loop(0, rows_b, final_row, 0)
 
@@ -491,14 +529,15 @@
                 pltpu.VMEM((rows + 2, cols + 2, imgs, ca), BF16),
                 pltpu.VMEM((rows_b + 2, cols_b + 2, imgs, cb), BF16),
                 pltpu.VMEM((rows, cols // 2 * imgs, 2 * ca), F32),
-                pltpu.VMEM((2, imgs * 17 + 16, 128), F32),
+                pltpu.VMEM((4, imgs * 17 + 16, 128), F32),
                 pltpu.VMEM((la, 12 * ca, 2 * ca), BF16),
                 pltpu.VMEM((9 * ca, cb), BF16),
                 pltpu.VMEM((lb, 9 * cb, cb), BF16),
                 pltpu.VMEM((rows, imgs, ca), BF16),
                 pltpu.VMEM((rows_b, imgs, cb), BF16),
                 pltpu.VMEM((layers, n_dev, 2, 256), F32),
-                dma((rows,)), dma((14,)),
+                pltpu.VMEM((lb + 1, (cols_b // 8 + 1) * imgs, 256), F32),
+                dma((rows,)), dma((14,)), dma((lb + 1,)), dma((lb + 1,)),
                 dma((2, NQ)), dma((2, NQ)), dma((3,)), dma((3,)), dma((layers, n_dev)), dma((layers, n_dev)),
             ],
             compiler_params=pltpu.CompilerParams(

time: 119 us -> 115 us (0.966)
  Pallas kernels: 116 us -> 112 us
    pallas_call x1, Pallas kernels: 116 us -> 112 us  [per_device(): pl.pallas_call(functools.partial(stack_kernel, dims), out_shape=pltpu.VME...]
where the time goes in v4:
time: 115 us; the launch traced here: 114 us
  Pallas kernels  112 us (97%)
  local copies, waits for them, and re-layouts  2.02 us (2%)
    pallas_call x1, Pallas kernels, per_device(): pl.pallas_call(functools.partial(stack_kernel, dims), out_shape=pltpu.VME...  112 us

profile of v4, /device:TPU:0, one launch (start us, length us, event | category | flops | bytes accessed | tf_op | source)
XLA Modules:
  0.0 114.5 jit_solution(2616573824677415232)
XLA Ops:
  0.0 112.4 %stack.1 = bf16[32,4,64,256]{3,2,1,0:T(8,128)(2,1)S(1)} custom-call(bf16[32,8,128,128]{3,2,1,0:T(8,128)(2,1)} %x_hbm.1, bf16[3,3,3,128,128]{4,3,2,1,0:T(8,128)(2,1)} %wa_hbm.1, f32[3,2,128]{2,1,0:T(2,128)} %bna_hbm.1, bf16[3,3,128,256]{3,2,1,0:T(8,128)(2,1)} %wd_ref.1, f32[2,256]{1,0:T(2,128)} %bnd_hbm.1, bf16[2,2304,256]{2,1,0:T(8,128)(2,1)} %bitcast.1, ...), custom_call_target="tpu_custom_call" | custom-call | tf_op jit(solution)/shard_map/stack/pallas_call | solution.py:520
  112.4 2.0 %copy.9 = bf16[32,4,64,256]{3,2,1,0:T(8,128)(2,1)} copy(bf16[32,4,64,256]{3,2,1,0:T(8,128)(2,1)S(1)} %stack.1) | data formatting | bytes 8388608

commit v5 on v4

--- a/solution.py
+++ b/solution.py
@@ -198,15 +198,18 @@
         x_copy(r).wait()
 
         def blk(c, carry):
-            c0 = pl.multiple_of(c * 16, 16)
-            for i in range(imgs):
-                stg[0, pl.ds(i * 17, 16), :] = xv[i, r, pl.ds(c0, 16), :].astype(F32)
-            for k in range(16):
-                z[r, pl.ds(pl.multiple_of(c * (8 * imgs), 8 * imgs) + (k // 2) * imgs, imgs),
-                  (k % 2) * ca:(k % 2 + 1) * ca] = stg[0, pl.ds(k, imgs, stride=17), :]
+            for g in range(2):
+                c0 = pl.multiple_of(c * 32 + g * 16, 16)
+                for i in range(imgs):
+                    stg[g, pl.ds(i * 17, 16), :] = xv[i, r, pl.ds(c0, 16), :].astype(F32)
+            for g in range(2):
+                base = pl.multiple_of((2 * c + g) * (8 * imgs), 8 * imgs)
+                for k in range(16):
+                    z[r, pl.ds(base + (k // 2) * imgs, imgs),
+                      (k % 2) * ca:(k % 2 + 1) * ca] = stg[g, pl.ds(k, imgs, stride=17), :]
             return carry
 
-        lax.fori_loop(0, cols // 16, blk, 0)
+        lax.fori_loop(0, cols // 32, blk, 0)
 
     def apply_bn(zz, aff):
         scale, shift, low = aff

time: 115 us -> 114 us (level)
  no operation moved by 1% of the time
where the time goes in v5:
time: 114 us
  Pallas kernels  112 us (98%)
  local copies, waits for them, and re-layouts  2.02 us (2%)
    pallas_call x1, Pallas kernels, per_device(): pl.pallas_call(functools.partial(stack_kernel, dims), out_shape=pltpu.VME...  112 us

profile of v5, /device:TPU:0, one launch (start us, length us, event | category | flops | bytes accessed | tf_op | source)
XLA Modules:
  0.0 113.9 jit_solution(7310892288759775852)
XLA Ops:
  0.0 111.8 %stack.1 = bf16[32,4,64,256]{3,2,1,0:T(8,128)(2,1)S(1)} custom-call(bf16[32,8,128,128]{3,2,1,0:T(8,128)(2,1)} %x_hbm.1, bf16[3,3,3,128,128]{4,3,2,1,0:T(8,128)(2,1)} %wa_hbm.1, f32[3,2,128]{2,1,0:T(2,128)} %bna_hbm.1, bf16[3,3,128,256]{3,2,1,0:T(8,128)(2,1)} %wd_ref.1, f32[2,256]{1,0:T(2,128)} %bnd_hbm.1, bf16[2,2304,256]{2,1,0:T(8,128)(2,1)} %bitcast.1, ...), custom_call_target="tpu_custom_call" | custom-call | tf_op jit(solution)/shard_map/stack/pallas_call | solution.py:523
  111.8 2.0 %copy.9 = bf16[32,4,64,256]{3,2,1,0:T(8,128)(2,1)} copy(bf16[32,4,64,256]{3,2,1,0:T(8,128)(2,1)S(1)} %stack.1) | data formatting | bytes 8388608
